TPU v7x, 32 devices: a whole 2x2x4 slice. The times are simulated.
32 devices in a mesh: tok: 16 (over z, y, core), lay: 2 (over x).
Axes of the slice: x: 2, y: 2, z: 4, core: 2. Of those that a mesh axis runs over, the one named last changes fastest.
Arguments:
- first_acts: bfloat16 [2, 4096, 5120], P('lay', 'tok'), may hold values from -40 to 40
- second_acts: bfloat16 [2, 4096, 5120], P('lay', 'tok'), may hold values from -40 to 40
Outputs:
- whitening: float32 [2, 2, 40, 128, 128], P(None, 'lay')
- similarity: float32 [2, 2, 40], P('lay')
All inputs are finite; a program needn't handle non-finite values.
Results may differ from a plain program's by a relative error of at most 0.0003.
Values may be sent and summed in bfloat16 or wider, within the bound.
A program may use at most 128 MiB of HBM per device.

v0:
```python
import functools

import jax
import jax.numpy as jnp
from jax import lax
from jax.experimental import pallas as pl
from jax.experimental.pallas import tpu as pltpu
from jax.sharding import PartitionSpec as P

HEADS = 40
HEAD_DIM = 128
ITERS = 6
PAD = 8

ridge_weight = 0.05
MESH = pl.DeviceIdType.MESH
HI = lax.Precision.HIGHEST


def dot_tt(a, b, precision=None):
    return lax.dot_general(
        a, b, (((0,), (0,)), ((), ())), preferred_element_type=jnp.float32, precision=precision
    )


def mm(a, b):
    return jnp.dot(a, b, preferred_element_type=jnp.float32, precision=HI)


BLOCKS = HEAD_DIM // 8
KEPT = BLOCKS // 2 + 1
PACKED = 8 * KEPT


def lane_block():
    return lax.broadcasted_iota(jnp.int32, (8, HEAD_DIM), 1) // 8


def pack(a):
    lb = lane_block()
    xs = [a[8 * e : 8 * e + 8, :] for e in range(BLOCKS)]
    step = 1
    while step < BLOCKS:
        bit = (lb // step) % 2 == 1
        xs = [jnp.where(bit, xs[(e + step) % BLOCKS], xs[e]) for e in range(BLOCKS)]
        step *= 2
    return jnp.concatenate([xs[(-d) % BLOCKS] for d in range(KEPT)], axis=0)


def unpack(p):
    lb = lane_block()
    zero = jnp.zeros((8, HEAD_DIM), jnp.float32)
    ys = [zero] * BLOCKS
    for d in range(KEPT):
        ys[(-d) % BLOCKS] = p[8 * d : 8 * d + 8, :]
    step = 1
    while step < BLOCKS:
        bit = (lb // step) % 2 == 1
        ys = [jnp.where(bit, ys[(e - step) % BLOCKS], ys[e]) for e in range(BLOCKS)]
        step *= 2
    half = jnp.concatenate(ys, axis=0)
    rb = lax.broadcasted_iota(jnp.int32, (HEAD_DIM, HEAD_DIM), 0) // 8
    cb = lax.broadcasted_iota(jnp.int32, (HEAD_DIM, HEAD_DIM), 1) // 8
    return jnp.where((cb - rb + BLOCKS) % BLOCKS < KEPT, half, half.T)


def kernel(
    n, R, hp, token_total,
    x1, x2, out, simout,
    x2o, gp, gd, gy, gz, cp, cd, cys, cy, czs, cz, slab, wbuf, wfull, sbuf, yb, zb,
    x_s, x_r, gd_s, gd_r, gy_s, gy_r, gz_s, gz_r,
    cd_s, cd_r, cy_s, cy_r, cz_s, cz_r,
    p_s, p_r, q_s, q_r, az_s, az_r, ay_s, ay_r, ad_s, ad_r, ss_s, ss_r, o_s,
):
    me = lax.axis_index("tok")
    lay = lax.axis_index("lay")
    other = 1 - lay
    c = lax.rem(me, 2)
    y = lax.rem(me // 2, 2)
    z = me // 4
    rows = x1.shape[0]
    D = HEAD_DIM
    core_peer = z * 4 + y * 2 + (1 - c)
    y_peer = z * 4 + (1 - y) * 2 + c

    def z_peer(zt):
        return zt * 4 + y * 2 + c

    def rc(src, dst, s, r, tok, ly):
        return pltpu.make_async_remote_copy(
            src_ref=src, dst_ref=dst, send_sem=s, recv_sem=r,
            device_id=(tok, ly), device_id_type=MESH,
        )

    barrier = pltpu.get_barrier_semaphore()
    for k in range(1, n):
        pl.semaphore_signal(barrier, inc=1, device_id=(lax.rem(me + k, n), lay), device_id_type=MESH)
    pl.semaphore_signal(barrier, inc=1, device_id=(me, other), device_id_type=MESH)
    pl.semaphore_wait(barrier, n)

    zts = [lax.rem(z + 1 + i, R) for i in range(R)]
    sends = []

    padded = R * 2 * hp != HEADS
    width = x1.shape[1] // R if not padded else x1.shape[1]
    x_parts = []
    for i in range(R if not padded else 1):
        cols = pl.ds(pl.multiple_of(zts[i] * width, 128), width) if not padded else pl.ds(0, width)
        d = rc(x2.at[:, cols], x2o.at[:, cols], x_s.at[i], x_r.at[i], me, other)
        d.start()
        x_parts.append(d)
        sends.append(d)

    def head_cols(zt, yy, j):
        h = (zt * 2 + yy) * hp + j
        if padded:
            h = jnp.minimum(h, HEADS - 1)
        return pl.ds(pl.multiple_of(h * D, D), D)

    ones = jnp.ones((PAD, rows), jnp.bfloat16)

    g_d = []
    for i in range(R):
        zt = zts[i]

        def gram_body(j, carry, zt=zt):
            for yy in range(2):
                cols = head_cols(zt, yy, j)
                for k, ref in enumerate((x1, x2)):
                    v = ref[:, cols]
                    gp[k, zt, yy, j, :PACKED, :] = pack(dot_tt(v, v))
                    gp[k, zt, yy, j, PACKED:, :] = jnp.dot(ones, v, preferred_element_type=jnp.float32)
            return carry

        lax.fori_loop(0, hp, gram_body, 0)
        d = rc(gp.at[1 - c, zt], gd.at[zt], gd_s.at[i], gd_r.at[i], core_peer, lay)
        d.start()
        g_d.append(d)
        sends.append(d)

    def y_phase(part, dbuf, ybuf, s, r, d_list):
        out_list = []
        for i in range(R):
            zt = zts[i]
            d_list[i].wait_recv()

            def add_body(j, carry, zt=zt):
                part[c, zt, 1 - y, j] = part[c, zt, 1 - y, j] + dbuf[zt, 1 - y, j]
                return carry

            lax.fori_loop(0, hp, add_body, 0)
            d = rc(part.at[c, zt, 1 - y], ybuf.at[zt], s.at[i], r.at[i], y_peer, lay)
            d.start()
            out_list.append(d)
            sends.append(d)
        return out_list

    def z_phase(part, dbuf, ybuf, zbuf, s, r, y_list):
        out_list = []
        for i in range(R):
            zt = zts[i]
            y_list[i].wait_recv()

            def add_body(j, carry, zt=zt):
                part[c, zt, y, j] = part[c, zt, y, j] + dbuf[zt, y, j] + ybuf[zt, j]
                return carry

            lax.fori_loop(0, hp, add_body, 0)
            if i < R - 1:
                d = rc(part.at[c, zt, y], zbuf.at[i], s.at[i], r.at[i], z_peer(zt), lay)
                d.start()
                out_list.append(d)
                sends.append(d)
        return out_list

    g_y = y_phase(gp, gd, gy, gy_s, gy_r, g_d)

    def c_d(i):
        return rc(cp.at[1 - c, zts[i]], cd.at[zts[i]], cd_s.at[i], cd_r.at[i], core_peer, lay)

    def c_y(i):
        return rc(cys.at[zts[i]], cy.at[zts[i]], cy_s.at[i], cy_r.at[i], y_peer, lay)

    def c_z(i):
        return rc(czs.at[zts[i]], cz.at[i], cz_s.at[i], cz_r.at[i], z_peer(zts[i]), lay)

    def cross_chunk(k, ref, i):
        zt = zts[i]

        def body(j, carry):
            for yy in range(2):
                cols = head_cols(zt, yy, j)
                cp[k, zt, yy, j] = dot_tt(x1[:, cols], ref[:, cols])
            return carry

        lax.fori_loop(0, hp, body, 0)

        @pl.when(c == 1 - k)
        def _():
            c_d(i).start()

    def cross_y(k):
        @pl.when(c == k)
        def _():
            for i in range(R):
                zt = zts[i]
                c_d(i).wait_recv()

                def body(j, carry, zt=zt):
                    total = cp[k, zt, 1 - y, j] + cd[zt, 1 - y, j]
                    cys[zt, j] = total
                    return carry

                lax.fori_loop(0, hp, body, 0)
                c_y(i).start()

    def cross_z(k):
        @pl.when(c == k)
        def _():
            for i in range(R):
                zt = zts[i]
                c_y(i).wait_recv()

                def body(j, carry, zt=zt, last=i == R - 1):
                    total = cp[k, zt, y, j] + cd[zt, y, j] + cy[zt, j]
                    if last:
                        cp[k, zt, y, j] = total
                    else:
                        czs[zt, j] = total
                    return carry

                lax.fori_loop(0, hp, body, 0)
                if i < R - 1:
                    c_z(i).start()

    for i in range(R):
        cross_chunk(0, x2, i)
    g_z = z_phase(gp, gd, gy, gz, gz_s, gz_r, g_y)
    cross_y(0)

    for d in g_z:
        d.wait_recv()

    eye = (
        lax.broadcasted_iota(jnp.int32, (D, D), 0) == lax.broadcasted_iota(jnp.int32, (D, D), 1)
    ).astype(jnp.float32)
    scales = []
    for j in range(hp):
        total = gp[c, z, y, j]
        for i in range(R - 1):
            total = total + gz[i, j]
        mean = total[PACKED:, :] / token_total
        slab[0, j, D:, :] = mean
        cov = unpack(total[:PACKED, :]) / token_total - dot_tt(mean, mean, HI) * (1.0 / PAD) + ridge_weight * eye
        norm2 = jnp.sum(jnp.sum(cov * cov, axis=1, keepdims=True), axis=0, keepdims=True)
        scale = jnp.sqrt(norm2)
        scales.append(scale)
        y0 = cov / scale
        f = 1.5 * eye - 0.5 * y0
        yb[j] = mm(y0, f)
        zb[j] = f

    def ns_body(t, carry):
        fs = [1.5 * eye - 0.5 * mm(zb[j], yb[j]) for j in range(hp)]
        for j in range(hp):
            yb[j] = mm(yb[j], fs[j])
            zb[j] = mm(fs[j], zb[j])
        return carry

    lax.fori_loop(1, ITERS - 1, ns_body, 0)
    for j in range(hp):
        f = 1.5 * eye - 0.5 * mm(zb[j], yb[j])
        w = mm(f, zb[j]) / jnp.sqrt(scales[j])
        slab[0, j, :D, :] = w
        wbuf[c, z, y, j] = pack(w)
        wfull[c, z, y, j] = w

    to_core = rc(slab.at[0], slab.at[1], p_s.at[0], p_r.at[0], core_peer, lay)
    to_lay = rc(slab.at[0], slab.at[2], q_s.at[0], q_r.at[0], me, other)
    to_core.start()
    to_lay.start()
    sends += [to_core, to_lay]

    a_z = []
    for i in range(R - 1):
        w_own = wbuf.at[c, z, y]
        d = rc(w_own, w_own, az_s.at[i], az_r.at[i], z_peer(zts[i]), lay)
        d.start()
        a_z.append(d)
        sends.append(d)

    def forward(e, zs):
        block = wbuf.at[c, zs, y]
        d = rc(block, block, ay_s.at[e], ay_r.at[e], y_peer, lay)
        d.start()
        f = rc(block, block, ad_s.at[2 * e], ad_r.at[2 * e], core_peer, lay)
        f.start()
        sends.extend([d, f])
        return d, f

    zss = [z] + [lax.rem(z + R - 1 - i, R) for i in range(R - 1)]
    a_y, a_d = [], []
    d, f = forward(0, z)
    a_y.append(d)
    a_d.append(f)

    outs = []

    def emit(cc, zs, yy):
        d = pltpu.make_async_copy(wfull.at[cc, zs, yy], out.at[cc, zs, yy], o_s.at[len(outs)])
        d.start()
        outs.append(d)

    def expand(cc, zs, yy):
        def body(j, carry):
            wfull[cc, zs, yy, j] = unpack(wbuf[cc, zs, yy, j])
            return carry

        lax.fori_loop(0, hp, body, 0)
        emit(cc, zs, yy)

    emit(c, z, y)
    cross_z(0)

    for i in range(R):
        if i < len(x_parts):
            x_parts[i].wait_recv()
        cross_chunk(1, x2o, i)
    cross_y(1)

    for i in range(R - 1):
        a_z[i].wait_recv()
        d, f = forward(i + 1, zss[i + 1])
        a_y.append(d)
        a_d.append(f)

    cross_z(1)

    for e in range(1, R):
        expand(c, zss[e], y)
    for e in range(R):
        a_y[e].wait_recv()
        block = wbuf.at[c, zss[e], 1 - y]
        f = rc(block, block, ad_s.at[2 * e + 1], ad_r.at[2 * e + 1], core_peer, lay)
        f.start()
        a_d.append(f)
        sends.append(f)
        expand(c, zss[e], 1 - y)

    for i in range(R - 1):
        c_z(i).wait_recv()
    to_core.wait_recv()
    to_lay.wait_recv()
    sub = lax.broadcasted_iota(jnp.int32, sbuf.shape[1:], 0)
    tile = jnp.zeros(sbuf.shape[1:], jnp.float32)
    for j in range(hp):
        total = cp[c, z, y, j]
        for i in range(R - 1):
            total = total + cz[i, j]
        left = slab[c, j]
        right = slab[1 + c, j]
        cross = total / token_total - dot_tt(left[D:, :], right[D:, :], HI) * (1.0 / PAD)
        white = mm(mm(left[:D, :], cross), right[:D, :])
        value = jnp.sum(jnp.sum(white * white, axis=1, keepdims=True), axis=0, keepdims=True) / HEAD_DIM
        tile = jnp.where(sub == j, value, tile)
    sbuf[me] = tile
    s_list = []
    for k in range(1, n):
        d = rc(sbuf.at[me], sbuf.at[me], ss_s.at[k], ss_r.at[k], lax.rem(me + k, n), lay)
        d.start()
        s_list.append(d)
        sends.append(d)

    for e in range(R):
        a_d[e].wait_recv()
        expand(1 - c, zss[e], y)
    for e in range(R):
        a_d[R + e].wait_recv()
        expand(1 - c, zss[e], 1 - y)
    for d in s_list:
        d.wait_recv()
    simout[...] = sbuf[...]
    for d in outs:
        d.wait()
    for d in sends:
        d.wait_send()
    for i in range(R):
        c_d(i).wait_send()
        c_y(i).wait_send()
    for i in range(R - 1):
        c_z(i).wait_send()


def solution(mesh):
    n = mesh.shape["tok"]
    R = n // 4
    hp = -(-HEADS // (n // 2))
    srows = -(-hp // 8) * 8
    D = HEAD_DIM
    E = PACKED + PAD

    def local(first_acts, second_acts):
        _, rows, width = first_acts.shape
        token_total = float(rows * n)
        f32 = jnp.float32
        dma = lambda k: pltpu.SemaphoreType.DMA((max(k, 1),))
        out, sims = pl.pallas_call(
            functools.partial(kernel, n, R, hp, token_total),
            out_shape=(
                jax.ShapeDtypeStruct((2, R, 2, hp, D, D), f32),
                jax.ShapeDtypeStruct((n, srows, D), f32),
            ),
            in_specs=[pl.BlockSpec(memory_space=pltpu.VMEM)] * 2,
            out_specs=(
                pl.BlockSpec(memory_space=pltpu.MemorySpace.HBM),
                pl.BlockSpec(memory_space=pltpu.VMEM),
            ),
            scratch_shapes=[
                pltpu.VMEM((rows, width), jnp.bfloat16),
                pltpu.VMEM((2, R, 2, hp, E, D), f32),
                pltpu.VMEM((R, 2, hp, E, D), f32),
                pltpu.VMEM((R, hp, E, D), f32),
                pltpu.VMEM((R - 1, hp, E, D), f32),
                pltpu.VMEM((2, R, 2, hp, D, D), f32),
                pltpu.VMEM((R, 2, hp, D, D), f32),
                pltpu.VMEM((R, hp, D, D), f32),
                pltpu.VMEM((R, hp, D, D), f32),
                pltpu.VMEM((R, hp, D, D), f32),
                pltpu.VMEM((R - 1, hp, D, D), f32),
                pltpu.VMEM((3, hp, D + PAD, D), f32),
                pltpu.VMEM((2, R, 2, hp, PACKED, D), f32),
                pltpu.VMEM((2, R, 2, hp, D, D), f32),
                pltpu.VMEM((n, srows, D), f32),
                pltpu.VMEM((hp, D, D), f32),
                pltpu.VMEM((hp, D, D), f32),
                dma(R), dma(R),
                dma(R), dma(R), dma(R), dma(R), dma(R - 1), dma(R - 1),
                dma(R), dma(R), dma(R), dma(R), dma(R - 1), dma(R - 1),
                dma(1), dma(1), dma(1), dma(1),
                dma(R - 1), dma(R - 1), dma(R), dma(R), dma(2 * R), dma(2 * R),
                dma(n), dma(n),
                dma(4 * R),
            ],
            compiler_params=pltpu.CompilerParams(
                collective_id=0, has_side_effects=True, vmem_limit_bytes=58 * 1024 * 1024
            ),
        )(first_acts[0], second_acts[0])
        whitening = out.reshape(2, R * 2 * hp, D, D)[:, None, :HEADS]
        s = sims[:, :hp, 0].reshape(R * 2, 2, hp).transpose(1, 0, 2).reshape(2, R * 2 * hp)[:, :HEADS]
        s = jnp.where(lax.axis_index("lay") == 0, s, s[::-1])
        return whitening, s[None]

    in_specs = (P("lay", "tok", None), P("lay", "tok", None))
    out_specs = (P(None, "lay", None, None, None), P("lay", None, None))
    return jax.shard_map(local, mesh=mesh, in_specs=in_specs, out_specs=out_specs, check_vma=False)
```

profile of v0, /device:TPU:0, one launch (start us, length us, event | category | flops | bytes accessed | tf_op | source)
XLA Modules:
  0.0 110.7 jit_solution(7356466058410058760)
XLA Ops:
  0.6 102.9 %shard_map.41 = (f32[2,4,2,5,128,128]{5,4,3,2,1,0:T(8,128)}, f32[16,8,128]{2,1,0:T(8,128)}) custom-call(bf16[256,5120]{1,0:T(8,128)(2,1)} %bitcast.11, bf16[256,5120]{1,0:T(8,128)(2,1)} %bitcast.12), custom_call_target="tpu_custom_call" | custom-call | tf_op jit(solution)/shard_map/pallas_call | solution.py:407
  103.6 0.9 slice_reduce_fusion
  104.5 0.1 reshape.7
  104.6 0.6 select_bitcast_fusion
  105.2 5.5 %copy.9 = f32[2,1,40,128,128]{4,3,2,1,0:T(8,128)} copy(f32[2,1,40,128,128]{4,3,2,1,0:T(8,128)} %bitcast.10) | data formatting | bytes 10485760
  (2 shorter events, 0.0 us)
where the time goes:
time: 113 us; the launch traced here: 111 us
  Pallas kernels  103 us (91%)
  local copies, waits for them, and re-layouts  6.53 us (6%)
    pallas_call x1, Pallas kernels, local(): pl.pallas_call(functools.partial(kernel, n, R, hp, token_total), out_shap...  103 us
    unnamed x1, local copies, waits for them, and re-layouts  5.49 us

commit v1 on v0

v1 whole, which is shorter than its diff:
```python
import functools

import jax
import jax.numpy as jnp
from jax import lax
from jax.experimental import pallas as pl
from jax.experimental.pallas import tpu as pltpu
from jax.sharding import PartitionSpec as P

HEADS = 40
HEAD_DIM = 128
ITERS = 6
PAD = 8

ridge_weight = 0.05
VMEM_LIMIT = 54 * 1024 * 1024
MESH = pl.DeviceIdType.MESH
HI = lax.Precision.HIGHEST


def dot_tt(a, b, precision=None):
    return lax.dot_general(
        a, b, (((0,), (0,)), ((), ())), preferred_element_type=jnp.float32, precision=precision
    )


def mm(a, b):
    return jnp.dot(a, b, preferred_element_type=jnp.float32, precision=HI)


BLOCKS = HEAD_DIM // 8
KEPT = BLOCKS // 2 + 1
PACKED = 8 * KEPT


def lane_block():
    return lax.broadcasted_iota(jnp.int32, (8, HEAD_DIM), 1) // 8


def pack(a):
    lb = lane_block()
    xs = [a[8 * e : 8 * e + 8, :] for e in range(BLOCKS)]
    step = 1
    while step < BLOCKS:
        bit = (lb // step) % 2 == 1
        xs = [jnp.where(bit, xs[(e + step) % BLOCKS], xs[e]) for e in range(BLOCKS)]
        step *= 2
    return jnp.concatenate([xs[(-d) % BLOCKS] for d in range(KEPT)], axis=0)


def unpack(p):
    lb = lane_block()
    zero = jnp.zeros((8, HEAD_DIM), jnp.float32)
    ys = [zero] * BLOCKS
    for d in range(KEPT):
        ys[(-d) % BLOCKS] = p[8 * d : 8 * d + 8, :]
    step = 1
    while step < BLOCKS:
        bit = (lb // step) % 2 == 1
        ys = [jnp.where(bit, ys[(e - step) % BLOCKS], ys[e]) for e in range(BLOCKS)]
        step *= 2
    half = jnp.concatenate(ys, axis=0)
    rb = lax.broadcasted_iota(jnp.int32, (HEAD_DIM, HEAD_DIM), 0) // 8
    cb = lax.broadcasted_iota(jnp.int32, (HEAD_DIM, HEAD_DIM), 1) // 8
    return jnp.where((cb - rb + BLOCKS) % BLOCKS < KEPT, half, half.T)


def kernel(
    n, R, hp, token_total,
    x1h, x2h, out, simout,
    x1, x2, x2o, gp, gd, gy, gz, cp, cd, cy, cz, slab, wbuf, sbuf, yb, zb,
    l_s, x_s, x_r, gd_s, gd_r, gy_s, gy_r, gz_s, gz_r,
    cd_s, cd_r, cy_s, cy_r, cz_s, cz_r,
    p_s, p_r, q_s, q_r, az_s, az_r, ay_s, ay_r, ad_s, ad_r, ss_s, ss_r,
):
    me = lax.axis_index("tok")
    lay = lax.axis_index("lay")
    other = 1 - lay
    c = lax.rem(me, 2)
    y = lax.rem(me // 2, 2)
    z = me // 4
    yn = 1 - y
    rows = x1.shape[0]
    D = HEAD_DIM
    core_peer = z * 4 + y * 2 + (1 - c)
    y_peer = z * 4 + yn * 2 + c
    padded = R * 2 * hp != HEADS

    def z_peer(zt):
        return zt * 4 + y * 2 + c

    def rc(src, dst, s, r, tok, ly):
        return pltpu.make_async_remote_copy(
            src_ref=src, dst_ref=dst, send_sem=s, recv_sem=r,
            device_id=(tok, ly), device_id_type=MESH,
        )

    def zt_of(i):
        return lax.rem(z + 1 + i, R)

    barrier = pltpu.get_barrier_semaphore()
    for k in range(1, n):
        pl.semaphore_signal(barrier, inc=1, device_id=(lax.rem(me + k, n), lay), device_id_type=MESH)
    pl.semaphore_signal(barrier, inc=1, device_id=(me, other), device_id_type=MESH)

    parts = 1 if padded else 2 * R
    width = x1.shape[1] // parts

    def part_cols(p):
        if padded:
            return pl.ds(0, width)
        half = yn if p % 2 == 0 else y
        return pl.ds(pl.multiple_of((zt_of(p // 2) * 2 + half) * width, 128), width)

    order = list(range(0, parts, 2)) + list(range(1, parts, 2))
    loads = {}
    for p in order:
        cols = part_cols(p)
        for k, (src, dst) in enumerate(((x2h, x2), (x1h, x1))):
            d = pltpu.make_async_copy(src.at[:, cols], dst.at[:, cols], l_s.at[2 * p + k])
            d.start()
            loads[p, k] = d

    def x_send(p):
        cols = part_cols(p)
        return rc(x2.at[:, cols], x2o.at[:, cols], x_s.at[p], x_r.at[p], me, other)

    pl.semaphore_wait(barrier, n)
    for p in range(parts):
        loads[p, 0].wait()
        x_send(p).start()
    for p in range(parts):
        loads[p, 1].wait()

    def head_cols(zt, yy, j):
        h = (zt * 2 + yy) * hp + j
        if padded:
            h = jnp.minimum(h, HEADS - 1)
        return pl.ds(pl.multiple_of(h * D, D), D)

    ones = jnp.ones((PAD, rows), jnp.bfloat16)

    def gram_half(i, half):
        zt = zt_of(i)
        yy = yn if half == 0 else y
        for j in range(hp):
            cols = head_cols(zt, yy, j)
            for k, ref in enumerate((x1, x2)):
                v = ref[:, cols]
                gp[k, zt, yy, j, :PACKED, :] = pack(dot_tt(v, v))
                gp[k, zt, yy, j, PACKED:, :] = jnp.dot(ones, v, preferred_element_type=jnp.float32)
        g_d(i, half).start()

    def g_d(i, half):
        zt = zt_of(i)
        yy = yn if half == 0 else y
        return rc(gp.at[1 - c, zt, yy], gd.at[zt, yy], gd_s.at[half, i], gd_r.at[half, i], core_peer, lay)

    def g_y(i):
        zt = zt_of(i)
        return rc(gp.at[c, zt, yn], gy.at[zt], gy_s.at[i], gy_r.at[i], y_peer, lay)

    def g_z(i):
        zt = zt_of(i)
        return rc(gp.at[c, zt, y], gz.at[i], gz_s.at[i], gz_r.at[i], z_peer(zt), lay)

    def g_yph(i):
        zt = zt_of(i)
        g_d(i, 0).wait_recv()
        for j in range(hp):
            gp[c, zt, yn, j] = gp[c, zt, yn, j] + gd[zt, yn, j]
        g_y(i).start()

    def g_zph(i, last):
        zt = zt_of(i)
        g_d(i, 1).wait_recv()
        g_y(i).wait_recv()
        for j in range(hp):
            gp[c, zt, y, j] = gp[c, zt, y, j] + gd[zt, y, j] + gy[zt, j]
        if not last:
            g_z(i).start()

    def first_body(i, carry):
        gram_half(i, 0)

        @pl.when(i >= 1)
        def _():
            g_yph(i - 1)

        return carry

    def second_body(i, carry):
        gram_half(i, 1)

        @pl.when(i == 0)
        def _():
            g_yph(R - 1)

        return carry

    lax.fori_loop(0, R, first_body, 0)
    lax.fori_loop(0, R, second_body, 0)

    def c_d(k, i, half):
        zt = zt_of(i)
        yy = yn if half == 0 else y
        return rc(cp.at[k, zt, yy], cd.at[zt, yy], cd_s.at[half, i], cd_r.at[half, i], core_peer, lay)

    def c_y(k, i):
        zt = zt_of(i)
        return rc(cp.at[k, zt, yn], cy.at[zt], cy_s.at[i], cy_r.at[i], y_peer, lay)

    def c_z(k, i):
        zt = zt_of(i)
        return rc(cp.at[k, zt, y], cz.at[i], cz_s.at[i], cz_r.at[i], z_peer(zt), lay)

    def cross_half(k, i, half):
        zt = zt_of(i)
        yy = yn if half == 0 else y
        ref = x2 if k == 0 else x2o
        for j in range(hp):
            cols = head_cols(zt, yy, j)
            cp[k, zt, yy, j] = dot_tt(x1[:, cols], ref[:, cols])

        @pl.when(c == 1 - k)
        def _():
            c_d(k, i, half).start()

    def cross_y(k, i):
        @pl.when(c == k)
        def _():
            zt = zt_of(i)
            c_d(k, i, 0).wait_recv()
            for j in range(hp):
                cp[k, zt, yn, j] = cp[k, zt, yn, j] + cd[zt, yn, j]
            c_y(k, i).start()

    def cross_z(k, i):
        @pl.when(c == k)
        def _():
            zt = zt_of(i)
            c_d(k, i, 1).wait_recv()
            c_y(k, i).wait_recv()
            for j in range(hp):
                cp[k, zt, y, j] = cp[k, zt, y, j] + cd[zt, y, j] + cy[zt, j]
            c_z(k, i).start()

    def loop(body, lo, hi):
        def step(i, carry):
            body(i)
            return carry

        lax.fori_loop(lo, hi, step, 0)

    def cross_own(half):
        def body(i):
            cross_half(0, i, half)

        loop(body, 0, R)

    def cross_other(i):
        for half in range(2):
            p = 2 * i + half
            if p < parts:
                x_send(p).wait_recv()
            cross_half(1, i, half)

    cross_own(0)
    g_zph(0, R == 1)
    cross_own(1)
    loop(lambda i: cross_y(0, i), 0, R)
    for i in range(1, R):
        g_zph(i, i == R - 1)
    cross_other(0)
    cross_y(1, 0)
    cross_z(0, 0)

    for i in range(R - 1):
        g_z(i).wait_recv()

    eye = (
        lax.broadcasted_iota(jnp.int32, (D, D), 0) == lax.broadcasted_iota(jnp.int32, (D, D), 1)
    ).astype(jnp.float32)
    scales = []
    for j in range(hp):
        total = gp[c, z, y, j]
        for i in range(R - 1):
            total = total + gz[i, j]
        mean = total[PACKED:, :] / token_total
        slab[0, j, D:, :] = mean
        cov = unpack(total[:PACKED, :]) / token_total - dot_tt(mean, mean, HI) * (1.0 / PAD) + ridge_weight * eye
        norm2 = jnp.sum(jnp.sum(cov * cov, axis=1, keepdims=True), axis=0, keepdims=True)
        scale = jnp.sqrt(norm2)
        scales.append(scale)
        y0 = cov / scale
        f = 1.5 * eye - 0.5 * y0
        yb[j] = mm(y0, f)
        zb[j] = f

    def ns_body(t, carry):
        fs = [1.5 * eye - 0.5 * mm(zb[j], yb[j]) for j in range(hp)]
        for j in range(hp):
            yb[j] = mm(yb[j], fs[j])
            zb[j] = mm(fs[j], zb[j])
        return carry

    lax.fori_loop(1, ITERS - 1, ns_body, 0)
    for j in range(hp):
        f = 1.5 * eye - 0.5 * mm(zb[j], yb[j])
        w = mm(f, zb[j]) / jnp.sqrt(scales[j])
        slab[0, j, :D, :] = w
        wbuf[c, z, y, j] = pack(w)
        out[c, z, y, j] = w

    def up(d):
        block = wbuf.at[c, z - d, y]
        return rc(block, block, az_s.at[0, d], az_r.at[0, d], z_peer(z + 1), lay)

    def down(d):
        block = wbuf.at[c, z + d, y]
        return rc(block, block, az_s.at[1, d], az_r.at[1, d], z_peer(z - 1), lay)

    def from_below(d):
        block = wbuf.at[c, z - d, y]
        return rc(block, block, az_s.at[0, d - 1], az_r.at[0, d - 1], z_peer(z - 1), lay)

    def from_above(d):
        block = wbuf.at[c, z + d, y]
        return rc(block, block, az_s.at[1, d - 1], az_r.at[1, d - 1], z_peer(z + 1), lay)

    def a_y(zs):
        block = wbuf.at[c, zs, y]
        return rc(block, block, ay_s.at[zs], ay_r.at[zs], y_peer, lay)

    def a_y_in(zs):
        block = wbuf.at[c, zs, yn]
        return rc(block, block, ay_s.at[zs], ay_r.at[zs], y_peer, lay)

    def a_d(cc, zs, half):
        block = wbuf.at[cc, zs, yn if half == 0 else y]
        return rc(block, block, ad_s.at[half, zs], ad_r.at[half, zs], core_peer, lay)

    to_core = rc(slab.at[0], slab.at[1], p_s.at[0], p_r.at[0], core_peer, lay)
    to_lay = rc(slab.at[0], slab.at[2], q_s.at[0], q_r.at[0], me, other)

    def has_below(d):
        return z - d >= 0

    def has_above(d):
        return z + d < R

    def when(cond):
        return pl.when(cond)

    @when(has_above(1))
    def _():
        up(0).start()

    @when(has_below(1))
    def _():
        down(0).start()

    a_y(z).start()
    to_core.start()
    a_d(c, z, 1).start()

    @pl.when(c == 1)
    def _():
        to_lay.start()

    def gather_z(d):
        @when(has_below(d))
        def _():
            from_below(d).wait_recv()

            @when(has_above(1))
            def _():
                up(d).start()

            a_y(z - d).start()
            a_d(c, z - d, 1).start()

        @when(has_above(d))
        def _():
            from_above(d).wait_recv()

            @when(has_below(1))
            def _():
                down(d).start()

            a_y(z + d).start()
            a_d(c, z + d, 1).start()

    def expand(cc, zs, yy):
        for j in range(hp):
            out[cc, zs, yy, j] = unpack(wbuf[cc, zs, yy, j])

    def sides(d, body):
        if d == 0:
            body(z)
            return

        @when(has_below(d))
        def _():
            body(z - d)

        @when(has_above(d))
        def _():
            body(z + d)

    def expand_z(d):
        sides(d, lambda zs: expand(c, zs, y))

    def gather_y(d):
        def body(zs):
            a_y_in(zs).wait_recv()
            a_d(c, zs, 0).start()
            expand(c, zs, yn)

        sides(d, body)

    def gather_core(d, half):
        def body(zs):
            a_d(1 - c, zs, half).wait_recv()
            expand(1 - c, zs, yn if half == 0 else y)

        sides(d, body)

    group = (z * 2 + y) * hp
    lane = lax.broadcasted_iota(jnp.int32, sbuf.shape[1:], 1)

    def s_out(k):
        return rc(sbuf.at[me], sbuf.at[me], ss_s.at[k], ss_r.at[k], lax.rem(me + k, n), lay)

    def s_in(k):
        src = lax.rem(me + n - k, n)
        return rc(sbuf.at[src], sbuf.at[src], ss_s.at[k], ss_r.at[k], src, lay)

    def final(k):
        @pl.when(c == k)
        def _():
            c_d(k, R - 1, 1).wait_recv()
            c_y(k, R - 1).wait_recv()
            for i in range(R - 1):
                c_z(k, i).wait_recv()
            to_core.wait_recv()
            if k == 1:
                to_lay.wait_recv()
            tile = jnp.zeros(sbuf.shape[1:], jnp.float32)
            for j in range(hp):
                total = cp[k, z, y, j] + cd[z, y, j] + cy[z, j]
                for i in range(R - 1):
                    total = total + cz[i, j]
                left = slab[k, j]
                right = slab[1 + k, j]
                cross = total / token_total - dot_tt(left[D:, :], right[D:, :], HI) * (1.0 / PAD)
                white = mm(mm(left[:D, :], cross), right[:D, :])
                value = jnp.sum(jnp.sum(white * white, axis=1, keepdims=True), axis=0, keepdims=True) / HEAD_DIM
                tile = jnp.where(lane == group + j, value, tile)
            sbuf[me] = tile
            for q in range(1, n):
                s_out(q).start()

    todo = []
    for i in range(1, R - 1):
        todo.append(lambda i=i: cross_z(0, i))
    own_steps = todo

    for f in own_steps:
        f()
    for i in range(1, R):
        cross_other(i)
        gather_z(i)
        cross_y(1, i)
        cross_z(1, i - 1)
        expand_z(i)
        gather_y(i - 1)
        if i == R - 2 or R == 2:
            final(0)
        gather_core(i - 1, 1)
    gather_y(R - 1)
    final(1)
    gather_core(R - 1, 1)
    for d in range(R):
        gather_core(d, 0)

    for k in range(1, n):
        s_in(k).wait_recv()
    row0 = sbuf[0]
    row1 = sbuf[1]
    for i in range(2, n, 2):
        row0 = row0 + sbuf[i]
        row1 = row1 + sbuf[i + 1]
    sub = lax.broadcasted_iota(jnp.int32, row0.shape, 0)
    simout[...] = jnp.where(sub == lay, row0, row1)[:2, :HEADS]

    for p in range(parts):
        x_send(p).wait_send()
    for i in range(R):
        for half in range(2):
            g_d(i, half).wait_send()
            c_d(1 - c, i, half).wait_send()
        g_y(i).wait_send()
        c_y(c, i).wait_send()
        a_y(i).wait_send()
        for half in range(2):
            a_d(c, i, half).wait_send()
    for i in range(R - 1):
        g_z(i).wait_send()
        c_z(c, i).wait_send()
    for d in range(R - 1):
        @when(jnp.logical_and(has_below(d), has_above(1)))
        def _():
            up(d).wait_send()

        @when(jnp.logical_and(has_above(d), has_below(1)))
        def _():
            down(d).wait_send()

    to_core.wait_send()

    @pl.when(c == 1)
    def _():
        to_lay.wait_send()

    for k in range(1, n):
        s_out(k).wait_send()


def solution(mesh):
    n = mesh.shape["tok"]
    R = n // 4
    hp = -(-HEADS // (n // 2))
    D = HEAD_DIM
    E = PACKED + PAD
    parts = 1 if R * 2 * hp != HEADS else 2 * R

    def local(first_acts, second_acts):
        _, rows, width = first_acts.shape
        token_total = float(rows * n)
        f32 = jnp.float32
        bf16 = jnp.bfloat16
        dma = lambda *k: pltpu.SemaphoreType.DMA(tuple(max(q, 1) for q in k))
        out, sims = pl.pallas_call(
            functools.partial(kernel, n, R, hp, token_total),
            out_shape=(
                pltpu.VMEM((2, R, 2, hp, D, D), f32),
                pltpu.VMEM((2, HEADS), f32),
            ),
            in_specs=[pl.BlockSpec(memory_space=pltpu.MemorySpace.HBM)] * 2,
            out_specs=(
                pl.BlockSpec(memory_space=pltpu.VMEM),
                pl.BlockSpec(memory_space=pltpu.VMEM),
            ),
            scratch_shapes=[
                pltpu.VMEM((rows, width), bf16),
                pltpu.VMEM((rows, width), bf16),
                pltpu.VMEM((rows, width), bf16),
                pltpu.VMEM((2, R, 2, hp, E, D), f32),
                pltpu.VMEM((R, 2, hp, E, D), f32),
                pltpu.VMEM((R, hp, E, D), f32),
                pltpu.VMEM((R - 1, hp, E, D), f32),
                pltpu.VMEM((2, R, 2, hp, D, D), f32),
                pltpu.VMEM((R, 2, hp, D, D), f32),
                pltpu.VMEM((R, hp, D, D), f32),
                pltpu.VMEM((R - 1, hp, D, D), f32),
                pltpu.VMEM((3, hp, D + PAD, D), f32),
                pltpu.VMEM((2, R, 2, hp, PACKED, D), f32),
                pltpu.VMEM((n, 8, D), f32),
                pltpu.VMEM((hp, D, D), f32),
                pltpu.VMEM((hp, D, D), f32),
                dma(2 * parts), dma(parts), dma(parts),
                dma(2, R), dma(2, R), dma(R), dma(R), dma(R - 1), dma(R - 1),
                dma(2, R), dma(2, R), dma(R), dma(R), dma(R - 1), dma(R - 1),
                dma(1), dma(1), dma(1), dma(1),
                dma(2, R), dma(2, R), dma(R), dma(R), dma(2, R), dma(2, R),
                dma(n), dma(n),
            ],
            compiler_params=pltpu.CompilerParams(
                collective_id=0, has_side_effects=True, vmem_limit_bytes=VMEM_LIMIT
            ),
        )(first_acts[0], second_acts[0])
        whitening = out.reshape(2, R * 2 * hp, D, D)[:, None, :HEADS]
        return whitening, sims[None]

    in_specs = (P("lay", "tok", None), P("lay", "tok", None))
    out_specs = (P(None, "lay", None, None, None), P("lay", None, None))
    return jax.shard_map(local, mesh=mesh, in_specs=in_specs, out_specs=out_specs, check_vma=False)
```

time: 113 us -> 90.6 us (0.80); the launches traced: 111 us -> 90.4 us
  Pallas kernels: 103 us -> 86.9 us
  local copies, waits for them, and re-layouts: 6.53 us -> 2.92 us
    pallas_call x1, Pallas kernels: 103 us -> 86.9 us  [local(): pl.pallas_call(functools.partial(kernel, n, R, hp, token_total), out_shap...]
    unnamed x1 -> x2, local copies, waits for them, and re-layouts: 5.49 us -> 2.92 us
where the time goes in v1:
time: 90.6 us; the launch traced here: 90.4 us
  Pallas kernels  86.9 us (96%)
  local copies, waits for them, and re-layouts  2.92 us (3%)
    pallas_call x1, Pallas kernels, local(): pl.pallas_call(functools.partial(kernel, n, R, hp, token_total), out_shap...  86.9 us
    unnamed x2, local copies, waits for them, and re-layouts  2.92 us

profile of v1, /device:TPU:0, one launch (start us, length us, event | category | flops | bytes accessed | tf_op | source)
XLA Modules:
  0.0 90.4 jit_solution(15969328032526880934)
XLA Ops:
  0.6 86.9 %shard_map.41 = (f32[2,4,2,5,128,128]{5,4,3,2,1,0:T(8,128)S(1)}, f32[2,40]{1,0:T(2,128)S(1)}) custom-call(bf16[256,5120]{1,0:T(8,128)(2,1)} %bitcast.8, bf16[256,5120]{1,0:T(8,128)(2,1)} %bitcast.9), custom_call_target="tpu_custom_call" | custom-call | tf_op jit(solution)/shard_map/pallas_call | solution.py:544
  87.5 2.4 %copy.7 = f32[2,1,40,128,128]{4,3,2,1,0:T(8,128)} copy(f32[2,1,40,128,128]{4,3,2,1,0:T(8,128)S(1)} %bitcast.6) | data formatting | bytes 10485760
  89.9 0.6 copy.8

commit v2 on v1

v2 whole, which is shorter than its diff:
```python
import functools

import jax
import jax.numpy as jnp
from jax import lax
from jax.experimental import pallas as pl
from jax.experimental.pallas import tpu as pltpu
from jax.sharding import PartitionSpec as P

HEADS = 40
HEAD_DIM = 128
ITERS = 6
PAD = 8

ridge_weight = 0.05
Z_FIRST = 2
VMEM_LIMIT = 54 * 1024 * 1024
MESH = pl.DeviceIdType.MESH
HI = lax.Precision.HIGHEST


def dot_tt(a, b, precision=None):
    return lax.dot_general(
        a, b, (((0,), (0,)), ((), ())), preferred_element_type=jnp.float32, precision=precision
    )


def mm(a, b):
    return jnp.dot(a, b, preferred_element_type=jnp.float32, precision=HI)


BLOCKS = HEAD_DIM // 8
KEPT = BLOCKS // 2 + 1
PACKED = 8 * KEPT


def lane_block():
    return lax.broadcasted_iota(jnp.int32, (8, HEAD_DIM), 1) // 8


def pack(a):
    lb = lane_block()
    xs = [a[8 * e : 8 * e + 8, :] for e in range(BLOCKS)]
    step = 1
    while step < BLOCKS:
        bit = (lb // step) % 2 == 1
        xs = [jnp.where(bit, xs[(e + step) % BLOCKS], xs[e]) for e in range(BLOCKS)]
        step *= 2
    return jnp.concatenate([xs[(-d) % BLOCKS] for d in range(KEPT)], axis=0)


def unpack(p):
    lb = lane_block()
    zero = jnp.zeros((8, HEAD_DIM), jnp.float32)
    ys = [zero] * BLOCKS
    for d in range(KEPT):
        ys[(-d) % BLOCKS] = p[8 * d : 8 * d + 8, :]
    step = 1
    while step < BLOCKS:
        bit = (lb // step) % 2 == 1
        ys = [jnp.where(bit, ys[(e - step) % BLOCKS], ys[e]) for e in range(BLOCKS)]
        step *= 2
    half = jnp.concatenate(ys, axis=0)
    rb = lax.broadcasted_iota(jnp.int32, (HEAD_DIM, HEAD_DIM), 0) // 8
    cb = lax.broadcasted_iota(jnp.int32, (HEAD_DIM, HEAD_DIM), 1) // 8
    return jnp.where((cb - rb + BLOCKS) % BLOCKS < KEPT, half, half.T)


def kernel(
    n, R, hp, zf, token_total,
    x1h, x2h, out, simout,
    x1, x2, x2o, gp, gd, gy, gz, cp, cd, cy, cz, cyf, czf, slab, wbuf, sbuf, yb, zb,
    l_s, x_s, x_r, gd_s, gd_r, gy_s, gy_r, gz_s, gz_r,
    cd_s, cd_r, cy_s, cy_r, cz_s, cz_r, fy_s, fy_r, fz_s, fz_r,
    p_s, p_r, q_s, q_r, az_s, az_r, ay_s, ay_r, ad_s, ad_r, ss_s, ss_r,
):
    me = lax.axis_index("tok")
    lay = lax.axis_index("lay")
    other = 1 - lay
    c = lax.rem(me, 2)
    y = lax.rem(me // 2, 2)
    z = me // 4
    yn = 1 - y
    rows = x1.shape[0]
    D = HEAD_DIM
    core_peer = z * 4 + y * 2 + (1 - c)
    y_peer = z * 4 + yn * 2 + c
    padded = R * 2 * hp != HEADS

    bits = [1 << t for t in range(R.bit_length() - 1)]

    def z_xor(o):
        total = 0
        for b in bits:
            zb = lax.rem(z // b, 2)
            ob = lax.rem(o // b, 2) if not isinstance(o, int) else o // b % 2
            total = total + b * (zb + ob - 2 * zb * ob)
        return total

    def z_peer(o):
        return z_xor(o) * 4 + y * 2 + c

    def terms_of(o):
        return [b for b in bits if o % (2 * b) == 0]

    def lowest(o):
        return next(b for b in bits if o // b % 2)

    def rc(src, dst, s, r, tok, ly):
        return pltpu.make_async_remote_copy(
            src_ref=src, dst_ref=dst, send_sem=s, recv_sem=r,
            device_id=(tok, ly), device_id_type=MESH,
        )

    def zt_of(i):
        return z_xor(R - 1 - i)

    barrier = pltpu.get_barrier_semaphore()
    for k in range(1, n):
        pl.semaphore_signal(barrier, inc=1, device_id=(lax.rem(me + k, n), lay), device_id_type=MESH)
    pl.semaphore_signal(barrier, inc=1, device_id=(me, other), device_id_type=MESH)

    parts = 1 if padded else 2 * R
    width = x1.shape[1] // parts

    def part_cols(p):
        if padded:
            return pl.ds(0, width)
        half = yn if p % 2 == 0 else y
        return pl.ds(pl.multiple_of((zt_of(p // 2) * 2 + half) * width, 128), width)

    order = list(range(0, parts, 2)) + list(range(1, parts, 2))
    loads = {}
    for p in order:
        cols = part_cols(p)
        for k, (src, dst) in enumerate(((x2h, x2), (x1h, x1))):
            d = pltpu.make_async_copy(src.at[:, cols], dst.at[:, cols], l_s.at[2 * p + k])
            d.start()
            loads[p, k] = d

    def x_send(p):
        cols = part_cols(p)
        return rc(x2.at[:, cols], x2o.at[:, cols], x_s.at[p], x_r.at[p], me, other)

    pl.semaphore_wait(barrier, n)
    for p in range(parts):
        loads[p, 0].wait()
        x_send(p).start()
    for p in range(parts):
        loads[p, 1].wait()

    def head_cols(zt, yy, j):
        h = (zt * 2 + yy) * hp + j
        if padded:
            h = jnp.minimum(h, HEADS - 1)
        return pl.ds(pl.multiple_of(h * D, D), D)

    ones = jnp.ones((PAD, rows), jnp.bfloat16)
    sub8 = lax.broadcasted_iota(jnp.int32, (PAD, D), 0)

    def gram_half(i, half):
        zt = zt_of(i)
        yy = yn if half == 0 else y
        sums = [jnp.zeros((PAD, D), jnp.float32)] * 2
        for j in range(hp):
            cols = head_cols(zt, yy, j)
            for k, ref in enumerate((x1, x2)):
                v = ref[:, cols]
                gp[k, zt, yy, j * PACKED : (j + 1) * PACKED, :] = pack(dot_tt(v, v))
                sums[k] = jnp.where(sub8 == j, jnp.dot(ones, v, preferred_element_type=jnp.float32), sums[k])
        for k in range(2):
            gp[k, zt, yy, hp * PACKED :, :] = sums[k]
        g_d(i, half).start()

    def g_d(i, half):
        zt = zt_of(i)
        yy = yn if half == 0 else y
        return rc(gp.at[1 - c, zt, yy], gd.at[zt, yy], gd_s.at[half, i], gd_r.at[half, i], core_peer, lay)

    def g_y(i):
        zt = zt_of(i)
        return rc(gp.at[c, zt, yn], gy.at[zt], gy_s.at[i], gy_r.at[i], y_peer, lay)

    def g_z(o, b):
        return rc(gp.at[c, z_xor(o), y], gz.at[o - 1], gz_s.at[o - 1], gz_r.at[o - 1], z_peer(b), lay)

    def g_yph(i):
        zt = zt_of(i)
        g_d(i, 0).wait_recv()
        gp[c, zt, yn] = gp[c, zt, yn] + gd[zt, yn]
        g_y(i).start()

    def g_zph(i):
        zt = zt_of(i)
        o = R - 1 - i
        g_d(i, 1).wait_recv()
        g_y(i).wait_recv()
        terms = terms_of(o) if o else []
        for b in terms:
            g_z(o + b, b).wait_recv()
        total = gp[c, zt, y] + gd[zt, y] + gy[zt]
        for b in terms:
            total = total + gz[o + b - 1]
        gp[c, zt, y] = total
        if o:
            g_z(o, lowest(o)).start()

    def first_body(i, carry):
        gram_half(i, 0)

        @pl.when(i >= 1)
        def _():
            g_yph(i - 1)

        return carry

    def second_body(i, carry):
        gram_half(i, 1)

        @pl.when(i == 0)
        def _():
            g_yph(R - 1)

        return carry

    lax.fori_loop(0, R, first_body, 0)
    lax.fori_loop(0, R, second_body, 0)

    def c_d(k, i, half):
        zt = zt_of(i)
        yy = yn if half == 0 else y
        return rc(cp.at[k, zt, yy], cd.at[zt, yy], cd_s.at[half, i], cd_r.at[half, i], core_peer, lay)

    def own_heads(k):
        return pl.ds(zf, hp - zf) if k == 0 else pl.ds(0, hp)

    def c_y(k, i):
        zt = zt_of(i)
        hs = own_heads(k)
        return rc(cp.at[k, zt, yn, hs], cy.at[zt, hs], cy_s.at[i], cy_r.at[i], y_peer, lay)

    def c_z(k, o, b):
        hs = own_heads(k)
        return rc(cp.at[k, z_xor(o), y, hs], cz.at[o - 1, hs], cz_s.at[o - 1], cz_r.at[o - 1], z_peer(b), lay)

    def f_z(o, b):
        return rc(
            cp.at[0, z_xor(o), :, pl.ds(0, zf)], czf.at[o - 1], fz_s.at[o - 1], fz_r.at[o - 1], z_peer(b), lay
        )

    def f_y():
        return rc(cp.at[0, z, yn, pl.ds(0, zf)], cyf, fy_s.at[0], fy_r.at[0], y_peer, lay)

    def first_z(i):
        @pl.when(c == 0)
        def _():
            o = R - 1 - i
            zt = zt_of(i)
            for b in terms_of(o):
                f_z(o + b, b).wait_recv()
            for half in range(2):
                for j in range(zf):
                    total = cp[0, zt, half, j]
                    for b in terms_of(o):
                        total = total + czf[o + b - 1, half, j]
                    cp[0, zt, half, j] = total
            if o:
                f_z(o, lowest(o)).start()
            else:
                f_y().start()

    def cross_half(k, i, half):
        zt = zt_of(i)
        yy = yn if half == 0 else y
        ref = x2 if k == 0 else x2o
        for j in range(hp):
            cols = head_cols(zt, yy, j)
            cp[k, zt, yy, j] = dot_tt(x1[:, cols], ref[:, cols])

        @pl.when(c == 1 - k)
        def _():
            c_d(k, i, half).start()

    def cross_y(k, i):
        @pl.when(c == k)
        def _():
            zt = zt_of(i)
            c_d(k, i, 0).wait_recv()
            for j in range(hp):
                cp[k, zt, yn, j] = cp[k, zt, yn, j] + cd[zt, yn, j]
            c_y(k, i).start()
            if k == 0:
                c_d(k, i, 1).wait_recv()
                for j in range(hp):
                    cp[k, zt, y, j] = cp[k, zt, y, j] + cd[zt, y, j]

    def cross_z(k, i):
        @pl.when(c == k)
        def _():
            zt = zt_of(i)
            o = R - 1 - i
            if k == 1:
                c_d(k, i, 1).wait_recv()
            c_y(k, i).wait_recv()
            terms = terms_of(o)
            for b in terms:
                c_z(k, o + b, b).wait_recv()
            for j in range(zf if k == 0 else 0, hp):
                total = cp[k, zt, y, j] + cy[zt, j]
                if k == 1:
                    total = total + cd[zt, y, j]
                for b in terms:
                    total = total + cz[o + b - 1, j]
                cp[k, zt, y, j] = total
            c_z(k, o, lowest(o)).start()

    def loop(body, lo, hi):
        def step(i, carry):
            body(i)
            return carry

        lax.fori_loop(lo, hi, step, 0)

    def cross_own(half):
        def body(i):
            cross_half(0, i, half)

        loop(body, 0, R)

    def cross_other(i, half):
        p = 2 * i + half
        if p < parts:
            x_send(p).wait_recv()
        cross_half(1, i, half)

    cross_own(0)
    cross_own(1)
    g_zph(0)
    loop(lambda i: cross_y(0, i), 0, R)
    first_z(0)
    for i in range(1, R - 1):
        g_zph(i)
    cross_other(0, 0)
    cross_other(0, 1)
    g_zph(R - 1)
    cross_y(1, 0)
    cross_z(0, 0)
    for i in range(1, R - 1):
        first_z(i)
    for b in bits:
        g_z(b, b).wait_recv()

    eye = (
        lax.broadcasted_iota(jnp.int32, (D, D), 0) == lax.broadcasted_iota(jnp.int32, (D, D), 1)
    ).astype(jnp.float32)
    scales = []
    tail = slice(hp * PACKED, hp * PACKED + PAD)
    col_sums = gp[c, z, y, tail, :]
    for b in bits:
        col_sums = col_sums + gz[b - 1, tail, :]
    for j in range(hp):
        at = slice(j * PACKED, (j + 1) * PACKED)
        total = gp[c, z, y, at, :]
        for b in bits:
            total = total + gz[b - 1, at, :]
        mean = jnp.where(sub8 == 0, col_sums[j : j + 1, :], 0.0) / token_total
        slab[0, j, D:, :] = mean
        cov = unpack(total) / token_total - dot_tt(mean, mean, HI) + ridge_weight * eye
        norm2 = jnp.sum(jnp.sum(cov * cov, axis=1, keepdims=True), axis=0, keepdims=True)
        scale = jnp.sqrt(norm2)
        scales.append(scale)
        y0 = cov / scale
        f = 1.5 * eye - 0.5 * y0
        yb[j] = mm(y0, f)
        zb[j] = f

    def ns_body(t, carry):
        fs = [1.5 * eye - 0.5 * mm(zb[j], yb[j]) for j in range(hp)]
        for j in range(hp):
            yb[j] = mm(yb[j], fs[j])
            zb[j] = mm(fs[j], zb[j])
        return carry

    lax.fori_loop(1, ITERS - 1, ns_body, 0)
    for j in range(hp):
        f = 1.5 * eye - 0.5 * mm(zb[j], yb[j])
        w = mm(f, zb[j]) / jnp.sqrt(scales[j])
        slab[0, j, :D, :] = w
        wbuf[c, z, y, j] = pack(w)
        out[c, z, y, j] = w

    def a_z(o, b):
        block = wbuf.at[c, z_xor(o), y]
        return rc(block, block, az_s.at[o + b], az_r.at[o + b], z_peer(b), lay)

    def a_z_in(o):
        block = wbuf.at[c, z_xor(o), y]
        return rc(block, block, az_s.at[o], az_r.at[o], z_peer(lowest(o)), lay)

    def a_y(o, half):
        block = wbuf.at[c, z_xor(o), yn if half == 0 else y]
        return rc(block, block, ay_s.at[o], ay_r.at[o], y_peer, lay)

    def a_d(cc, o, half):
        block = wbuf.at[cc, z_xor(o), yn if half == 0 else y]
        return rc(block, block, ad_s.at[half, o], ad_r.at[half, o], core_peer, lay)

    to_core = rc(slab.at[0], slab.at[1], p_s.at[0], p_r.at[0], core_peer, lay)
    to_lay = rc(slab.at[0], slab.at[2], q_s.at[0], q_r.at[0], me, other)

    def forward(o):
        for b in terms_of(o):
            a_z(o, b).start()
        a_y(o, 1).start()
        a_d(c, o, 1).start()

    def expand(cc, o, yy):
        zs = z_xor(o)
        for j in range(hp):
            out[cc, zs, yy, j] = unpack(wbuf[cc, zs, yy, j])

    def gather_z(o):
        a_z_in(o).wait_recv()
        forward(o)

    def expand_z(o):
        expand(c, o, y)

    def gather_y(o):
        a_y(o, 0).wait_recv()
        a_d(c, o, 0).start()
        expand(c, o, yn)

    def gather_core(o, half):
        a_d(1 - c, o, half).wait_recv()
        expand(1 - c, o, yn if half == 0 else y)

    forward(0)
    to_core.start()

    @pl.when(c == 1)
    def _():
        to_lay.start()

    group = (z * 2 + y) * hp
    lane = lax.broadcasted_iota(jnp.int32, sbuf.shape[1:], 1)

    def s_out(k):
        return rc(sbuf.at[me], sbuf.at[me], ss_s.at[k], ss_r.at[k], lax.rem(me + k, n), lay)

    def s_in(k):
        src = lax.rem(me + n - k, n)
        return rc(sbuf.at[src], sbuf.at[src], ss_s.at[k], ss_r.at[k], src, lay)

    def final(k):
        @pl.when(c == k)
        def _():
            if k == 0:
                f_y().wait_recv()
            else:
                c_d(k, R - 1, 1).wait_recv()
            c_y(k, R - 1).wait_recv()
            for b in bits:
                c_z(k, b, b).wait_recv()
            to_core.wait_recv()
            if k == 1:
                to_lay.wait_recv()
            tile = jnp.zeros(sbuf.shape[1:], jnp.float32)
            for j in range(hp):
                if k == 0 and j < zf:
                    total = cp[k, z, y, j] + cyf[j]
                else:
                    total = cp[k, z, y, j] + cy[z, j]
                    if k == 1:
                        total = total + cd[z, y, j]
                    for b in bits:
                        total = total + cz[b - 1, j]
                left = slab[k, j]
                right = slab[1 + k, j]
                cross = total / token_total - dot_tt(left[D:, :], right[D:, :], HI)
                white = mm(mm(left[:D, :], cross), right[:D, :])
                value = jnp.sum(jnp.sum(white * white, axis=1, keepdims=True), axis=0, keepdims=True) / HEAD_DIM
                tile = jnp.where(lane == group + j, value, tile)
            sbuf[me] = tile
            for q in range(1, n):
                s_out(q).start()

    for i in range(1, R - 1):
        cross_z(0, i)
    cross_z(1, 0)
    steps = sorted(range(1, R), key=lambda o: (bin(o).count("1"), o))
    lag = [0]
    seen = []
    for i in range(1, R - 1):
        new = steps[-(-(R - 1) * (i - 1) // (R - 2)) : -(-(R - 1) * i // (R - 2))]
        cross_other(i, 0)
        if i > 1:
            cross_z(1, i - 1)
        cross_other(i, 1)
        cross_y(1, i)
        if i == 1:
            first_z(R - 1)
        gather_z(new[0])
        for o in lag:
            gather_y(o)
        for o in new[1:]:
            gather_z(o)
        for o in new:
            expand_z(o)
        seen += lag
        lag = new
    final(0)
    cross_other(R - 1, 0)
    cross_z(1, R - 2)
    cross_y(1, R - 1)
    for o in seen:
        gather_core(o, 1)
    for o in lag:
        gather_y(o)
    cross_other(R - 1, 1)
    for o in lag:
        gather_core(o, 1)
    final(1)
    for o in seen + lag:
        gather_core(o, 0)

    for k in range(1, n):
        s_in(k).wait_recv()
    row0 = sbuf[0]
    row1 = sbuf[1]
    for i in range(2, n, 2):
        row0 = row0 + sbuf[i]
        row1 = row1 + sbuf[i + 1]
    sub = lax.broadcasted_iota(jnp.int32, row0.shape, 0)
    simout[...] = jnp.where(sub == lay, row0, row1)[:2, :HEADS]

    for p in range(parts):
        x_send(p).wait_send()
    for i in range(R):
        for half in range(2):
            g_d(i, half).wait_send()
            c_d(1 - c, i, half).wait_send()
        g_y(i).wait_send()
        for k in range(2):
            @pl.when(c == k)
            def _():
                c_y(k, i).wait_send()

        a_y(i, 1).wait_send()
        for half in range(2):
            a_d(c, i, half).wait_send()
    for o in range(R):
        if o:
            g_z(o, lowest(o)).wait_send()

            @pl.when(c == 0)
            def _():
                c_z(0, o, lowest(o)).wait_send()
                f_z(o, lowest(o)).wait_send()

            @pl.when(c == 1)
            def _():
                c_z(1, o, lowest(o)).wait_send()
        for b in bits:
            if b in terms_of(o):
                a_z(o, b).wait_send()

    to_core.wait_send()

    @pl.when(c == 0)
    def _():
        f_y().wait_send()

    @pl.when(c == 1)
    def _():
        to_lay.wait_send()

    for k in range(1, n):
        s_out(k).wait_send()


def solution(mesh):
    n = mesh.shape["tok"]
    R = n // 4
    hp = -(-HEADS // (n // 2))
    zf = max(hp * Z_FIRST // 5, 1)
    D = HEAD_DIM
    E = hp * PACKED + PAD
    parts = 1 if R * 2 * hp != HEADS else 2 * R

    def local(first_acts, second_acts):
        _, rows, width = first_acts.shape
        token_total = float(rows * n)
        f32 = jnp.float32
        bf16 = jnp.bfloat16
        dma = lambda *k: pltpu.SemaphoreType.DMA(tuple(max(q, 1) for q in k))
        out, sims = pl.pallas_call(
            functools.partial(kernel, n, R, hp, zf, token_total),
            out_shape=(
                pltpu.VMEM((2, R, 2, hp, D, D), f32),
                pltpu.VMEM((2, HEADS), f32),
            ),
            in_specs=[pl.BlockSpec(memory_space=pltpu.MemorySpace.HBM)] * 2,
            out_specs=(
                pl.BlockSpec(memory_space=pltpu.VMEM),
                pl.BlockSpec(memory_space=pltpu.VMEM),
            ),
            scratch_shapes=[
                pltpu.VMEM((rows, width), bf16),
                pltpu.VMEM((rows, width), bf16),
                pltpu.VMEM((rows, width), bf16),
                pltpu.VMEM((2, R, 2, E, D), f32),
                pltpu.VMEM((R, 2, E, D), f32),
                pltpu.VMEM((R, E, D), f32),
                pltpu.VMEM((R - 1, E, D), f32),
                pltpu.VMEM((2, R, 2, hp, D, D), f32),
                pltpu.VMEM((R, 2, hp, D, D), f32),
                pltpu.VMEM((R, hp, D, D), f32),
                pltpu.VMEM((R - 1, hp, D, D), f32),
                pltpu.VMEM((zf, D, D), f32),
                pltpu.VMEM((R - 1, 2, zf, D, D), f32),
                pltpu.VMEM((3, hp, D + PAD, D), f32),
                pltpu.VMEM((2, R, 2, hp, PACKED, D), f32),
                pltpu.VMEM((n, 8, D), f32),
                pltpu.VMEM((hp, D, D), f32),
                pltpu.VMEM((hp, D, D), f32),
                dma(2 * parts), dma(parts), dma(parts),
                dma(2, R), dma(2, R), dma(R), dma(R), dma(R - 1), dma(R - 1),
                dma(2, R), dma(2, R), dma(R), dma(R), dma(R - 1), dma(R - 1), dma(1), dma(1), dma(R - 1), dma(R - 1),
                dma(1), dma(1), dma(1), dma(1),
                dma(R), dma(R), dma(R), dma(R), dma(2, R), dma(2, R),
                dma(n), dma(n),
            ],
            compiler_params=pltpu.CompilerParams(
                collective_id=0, has_side_effects=True, vmem_limit_bytes=VMEM_LIMIT
            ),
        )(first_acts[0], second_acts[0])
        whitening = out.reshape(2, R * 2 * hp, D, D)[:, None, :HEADS]
        return whitening, sims[None]

    in_specs = (P("lay", "tok", None), P("lay", "tok", None))
    out_specs = (P(None, "lay", None, None, None), P("lay", None, None))
    return jax.shard_map(local, mesh=mesh, in_specs=in_specs, out_specs=out_specs, check_vma=False)
```

time: 90.6 us -> 82.7 us (0.913)
  Pallas kernels: 86.9 us -> 79 us
    pallas_call x1, Pallas kernels: 86.9 us -> 79 us  [local(): pl.pallas_call(functools.partial(kernel, n, R, hp, zf, token_total), out_...]
where the time goes in v2:
time: 82.7 us; the launch traced here: 82.5 us
  Pallas kernels  79 us (96%)
  local copies, waits for them, and re-layouts  2.92 us (4%)
    pallas_call x1, Pallas kernels, local(): pl.pallas_call(functools.partial(kernel, n, R, hp, zf, token_total), out_...  79 us
    unnamed x2, local copies, waits for them, and re-layouts  2.92 us

profile of v2, /device:TPU:0, one launch (start us, length us, event | category | flops | bytes accessed | tf_op | source)
XLA Modules:
  0.0 82.5 jit_solution(12879641114446466907)
XLA Ops:
  0.6 79.0 %shard_map.41 = (f32[2,4,2,5,128,128]{5,4,3,2,1,0:T(8,128)S(1)}, f32[2,40]{1,0:T(2,128)S(1)}) custom-call(bf16[256,5120]{1,0:T(8,128)(2,1)} %bitcast.8, bf16[256,5120]{1,0:T(8,128)(2,1)} %bitcast.9), custom_call_target="tpu_custom_call" | custom-call | tf_op jit(solution)/shard_map/pallas_call | solution.py:597
  79.6 2.4 %copy.7 = f32[2,1,40,128,128]{4,3,2,1,0:T(8,128)} copy(f32[2,1,40,128,128]{4,3,2,1,0:T(8,128)S(1)} %bitcast.6) | data formatting | bytes 10485760
  82.0 0.6 copy.8

commit v3 on v1

--- a/solution.py
+++ b/solution.py
@@ -13,6 +13,7 @@
 PAD = 8
 
 ridge_weight = 0.05
+Z_FIRST = 2
 VMEM_LIMIT = 54 * 1024 * 1024
 MESH = pl.DeviceIdType.MESH
 HI = lax.Precision.HIGHEST
@@ -66,11 +67,11 @@
 
 
 def kernel(
-    n, R, hp, token_total,
+    n, R, hp, zf, token_total,
     x1h, x2h, out, simout,
-    x1, x2, x2o, gp, gd, gy, gz, cp, cd, cy, cz, slab, wbuf, sbuf, yb, zb,
+    x1, x2, x2o, gp, gd, gy, gz, cp, cd, cy, cz, cyf, czf, slab, wbuf, sbuf, yb, zb,
     l_s, x_s, x_r, gd_s, gd_r, gy_s, gy_r, gz_s, gz_r,
-    cd_s, cd_r, cy_s, cy_r, cz_s, cz_r,
+    cd_s, cd_r, cy_s, cy_r, cz_s, cz_r, fy_s, fy_r, fz_s, fz_r,
     p_s, p_r, q_s, q_r, az_s, az_r, ay_s, ay_r, ad_s, ad_r, ss_s, ss_r,
 ):
     me = lax.axis_index("tok")
@@ -86,8 +87,57 @@
     y_peer = z * 4 + yn * 2 + c
     padded = R * 2 * hp != HEADS
 
-    def z_peer(zt):
+    bits = [1 << t for t in range(R.bit_length() - 1)]
+
+    def z_xor(o):
+        total = 0
+        for b in bits:
+            zb = lax.rem(z // b, 2)
+            ob = lax.rem(o // b, 2) if not isinstance(o, int) else o // b % 2
+            total = total + b * (zb + ob - 2 * zb * ob)
+        return total
+
+    def z_peer_at(zt):
         return zt * 4 + y * 2 + c
+
+    def z_peer(o):
+        return z_xor(o) * 4 + y * 2 + c
+
+    def at_least(a, b):
+        return (a - b + R) // R
+
+    def ct_of(i):
+        step = R - 1 - i
+        below = z
+        above = R - 1 - z
+        short = jnp.minimum(below, above)
+        up_far = at_least(above, below)
+        paired = 1 - at_least(step, 2 * short + 1)
+        dist = paired * ((step + 1) // 2) + (1 - paired) * (step - short)
+        near_side = paired * (1 - lax.rem(step, 2))
+        up = up_far + near_side - 2 * up_far * near_side
+        return z + dist * (2 * up - 1)
+
+    def hop(zt):
+        return 2 * at_least(zt, z) - 1
+
+    def slot_of(zt):
+        direction = hop(zt)
+        last = (R - direction * (zt - z)) // (R - 1)
+        down = (1 - direction) // 2
+        return zt + (R - zt) * last * down
+
+    def has_source(zt):
+        return inside(z - hop(zt))
+
+    def inside(q):
+        return at_least(q, 0) * at_least(R - 1, q)
+
+    def terms_of(o):
+        return [b for b in bits if o % (2 * b) == 0]
+
+    def lowest(o):
+        return next(b for b in bits if o // b % 2)
 
     def rc(src, dst, s, r, tok, ly):
         return pltpu.make_async_remote_copy(
@@ -96,7 +146,7 @@
         )
 
     def zt_of(i):
-        return lax.rem(z + 1 + i, R)
+        return z_xor(R - 1 - i)
 
     barrier = pltpu.get_barrier_semaphore()
     for k in range(1, n):
@@ -110,7 +160,7 @@
         if padded:
             return pl.ds(0, width)
         half = yn if p % 2 == 0 else y
-        return pl.ds(pl.multiple_of((zt_of(p // 2) * 2 + half) * width, 128), width)
+        return pl.ds(pl.multiple_of((ct_of(p // 2) * 2 + half) * width, 128), width)
 
     order = list(range(0, parts, 2)) + list(range(1, parts, 2))
     loads = {}
@@ -139,16 +189,20 @@
         return pl.ds(pl.multiple_of(h * D, D), D)
 
     ones = jnp.ones((PAD, rows), jnp.bfloat16)
+    sub8 = lax.broadcasted_iota(jnp.int32, (PAD, D), 0)
 
     def gram_half(i, half):
         zt = zt_of(i)
         yy = yn if half == 0 else y
+        sums = [jnp.zeros((PAD, D), jnp.float32)] * 2
         for j in range(hp):
             cols = head_cols(zt, yy, j)
             for k, ref in enumerate((x1, x2)):
                 v = ref[:, cols]
-                gp[k, zt, yy, j, :PACKED, :] = pack(dot_tt(v, v))
-                gp[k, zt, yy, j, PACKED:, :] = jnp.dot(ones, v, preferred_element_type=jnp.float32)
+                gp[k, zt, yy, j * PACKED : (j + 1) * PACKED, :] = pack(dot_tt(v, v))
+                sums[k] = jnp.where(sub8 == j, jnp.dot(ones, v, preferred_element_type=jnp.float32), sums[k])
+        for k in range(2):
+            gp[k, zt, yy, hp * PACKED :, :] = sums[k]
         g_d(i, half).start()
 
     def g_d(i, half):
@@ -160,25 +214,29 @@
         zt = zt_of(i)
         return rc(gp.at[c, zt, yn], gy.at[zt], gy_s.at[i], gy_r.at[i], y_peer, lay)
 
-    def g_z(i):
-        zt = zt_of(i)
-        return rc(gp.at[c, zt, y], gz.at[i], gz_s.at[i], gz_r.at[i], z_peer(zt), lay)
+    def g_z(o, b):
+        return rc(gp.at[c, z_xor(o), y], gz.at[o - 1], gz_s.at[o - 1], gz_r.at[o - 1], z_peer(b), lay)
 
     def g_yph(i):
         zt = zt_of(i)
         g_d(i, 0).wait_recv()
-        for j in range(hp):
-            gp[c, zt, yn, j] = gp[c, zt, yn, j] + gd[zt, yn, j]
+        gp[c, zt, yn] = gp[c, zt, yn] + gd[zt, yn]
         g_y(i).start()
 
-    def g_zph(i, last):
+    def g_zph(i):
         zt = zt_of(i)
+        o = R - 1 - i
         g_d(i, 1).wait_recv()
         g_y(i).wait_recv()
-        for j in range(hp):
-            gp[c, zt, y, j] = gp[c, zt, y, j] + gd[zt, y, j] + gy[zt, j]
-        if not last:
-            g_z(i).start()
+        terms = terms_of(o) if o else []
+        for b in terms:
+            g_z(o + b, b).wait_recv()
+        total = gp[c, zt, y] + gd[zt, y] + gy[zt]
+        for b in terms:
+            total = total + gz[o + b - 1]
+        gp[c, zt, y] = total
+        if o:
+            g_z(o, lowest(o)).start()
 
     def first_body(i, carry):
         gram_half(i, 0)
@@ -199,23 +257,70 @@
         return carry
 
     lax.fori_loop(0, R, first_body, 0)
-    lax.fori_loop(0, R, second_body, 0)
 
     def c_d(k, i, half):
-        zt = zt_of(i)
+        zt = ct_of(i)
         yy = yn if half == 0 else y
         return rc(cp.at[k, zt, yy], cd.at[zt, yy], cd_s.at[half, i], cd_r.at[half, i], core_peer, lay)
 
+    def own_heads(k):
+        return pl.ds(zf, hp - zf) if k == 0 else pl.ds(0, hp)
+
     def c_y(k, i):
-        zt = zt_of(i)
-        return rc(cp.at[k, zt, yn], cy.at[zt], cy_s.at[i], cy_r.at[i], y_peer, lay)
-
-    def c_z(k, i):
-        zt = zt_of(i)
-        return rc(cp.at[k, zt, y], cz.at[i], cz_s.at[i], cz_r.at[i], z_peer(zt), lay)
+        zt = ct_of(i)
+        hs = own_heads(k)
+        return rc(cp.at[k, zt, yn, hs], cy.at[zt, hs], cy_s.at[i], cy_r.at[i], y_peer, lay)
+
+    def c_z(k, zt, slot):
+        hs = own_heads(k)
+        return rc(cp.at[k, zt, y, hs], cz.at[slot, hs], cz_s.at[zt], cz_r.at[slot], z_peer_at(z + hop(zt)), lay)
+
+    def c_z_in(k, slot):
+        hs = own_heads(k)
+        return rc(cp.at[k, z, y, hs], cz.at[slot, hs], cz_s.at[z], cz_r.at[slot], me, other)
+
+    def f_z(zt, slot):
+        return rc(
+            cp.at[0, zt, :, pl.ds(0, zf)], czf.at[slot], fz_s.at[zt], fz_r.at[slot], z_peer_at(z + hop(zt)), lay
+        )
+
+    def f_z_in(slot):
+        return rc(cp.at[0, z, :, pl.ds(0, zf)], czf.at[slot], fz_s.at[z], fz_r.at[slot], me, other)
+
+    def f_y():
+        return rc(cp.at[0, z, yn, pl.ds(0, zf)], cyf, fy_s.at[0], fy_r.at[0], y_peer, lay)
+
+    def sources(zt, own, body):
+        if own:
+            pl.when(z > 0)(lambda: body(z))
+            pl.when(z < R - 1)(lambda: body(R))
+        else:
+            pl.when(has_source(zt) == 1)(lambda: body(zt))
+
+    def first_z(i, chained=None):
+        ready = c == 0
+        if chained is not None:
+            ready = jnp.logical_and(ready, has_source(ct_of(i)) == chained)
+
+        @pl.when(ready)
+        def _():
+            own = i == R - 1
+            zt = ct_of(i)
+
+            def add(slot):
+                f_z_in(slot).wait_recv()
+                for half in range(2):
+                    for j in range(zf):
+                        cp[0, zt, half, j] = cp[0, zt, half, j] + czf[slot, half, j]
+
+            sources(zt, own, add)
+            if own:
+                f_y().start()
+            else:
+                f_z(zt, slot_of(zt)).start()
 
     def cross_half(k, i, half):
-        zt = zt_of(i)
+        zt = ct_of(i)
         yy = yn if half == 0 else y
         ref = x2 if k == 0 else x2o
         for j in range(hp):
@@ -229,21 +334,36 @@
     def cross_y(k, i):
         @pl.when(c == k)
         def _():
-            zt = zt_of(i)
+            zt = ct_of(i)
             c_d(k, i, 0).wait_recv()
             for j in range(hp):
                 cp[k, zt, yn, j] = cp[k, zt, yn, j] + cd[zt, yn, j]
             c_y(k, i).start()
-
-    def cross_z(k, i):
-        @pl.when(c == k)
-        def _():
-            zt = zt_of(i)
-            c_d(k, i, 1).wait_recv()
+            if k == 0:
+                c_d(k, i, 1).wait_recv()
+                for j in range(hp):
+                    cp[k, zt, y, j] = cp[k, zt, y, j] + cd[zt, y, j]
+
+    def cross_z(k, i, chained):
+        @pl.when(jnp.logical_and(c == k, has_source(ct_of(i)) == chained))
+        def _():
+            zt = ct_of(i)
+            if k == 1:
+                c_d(k, i, 1).wait_recv()
             c_y(k, i).wait_recv()
-            for j in range(hp):
-                cp[k, zt, y, j] = cp[k, zt, y, j] + cd[zt, y, j] + cy[zt, j]
-            c_z(k, i).start()
+            for j in range(zf if k == 0 else 0, hp):
+                total = cp[k, zt, y, j] + cy[zt, j]
+                if k == 1:
+                    total = total + cd[zt, y, j]
+                cp[k, zt, y, j] = total
+
+            def add(slot):
+                c_z_in(k, slot).wait_recv()
+                for j in range(zf if k == 0 else 0, hp):
+                    cp[k, zt, y, j] = cp[k, zt, y, j] + cz[slot, j]
+
+            sources(zt, False, add)
+            c_z(k, zt, slot_of(zt)).start()
 
     def loop(body, lo, hi):
         def step(i, carry):
@@ -252,43 +372,51 @@
 
         lax.fori_loop(lo, hi, step, 0)
 
-    def cross_own(half):
-        def body(i):
-            cross_half(0, i, half)
-
-        loop(body, 0, R)
-
-    def cross_other(i):
-        for half in range(2):
-            p = 2 * i + half
-            if p < parts:
-                x_send(p).wait_recv()
-            cross_half(1, i, half)
+    def cross_own(i):
+        cross_half(0, i, 0)
+        cross_half(0, i, 1)
+
+    def cross_other(i, half):
+        p = 2 * i + half
+        if p < parts:
+            x_send(p).wait_recv()
+        cross_half(1, i, half)
 
     cross_own(0)
-    g_zph(0, R == 1)
-    cross_own(1)
-    loop(lambda i: cross_y(0, i), 0, R)
-    for i in range(1, R):
-        g_zph(i, i == R - 1)
-    cross_other(0)
+    lax.fori_loop(0, R, second_body, 0)
+    cross_y(0, 0)
+    first_z(0, 0)
+    loop(cross_own, 1, R)
+    g_zph(0)
+    loop(lambda i: cross_y(0, i), 1, R)
+    for i in range(1, R - 1):
+        g_zph(i)
+        if i == 1:
+            first_z(0, 1)
+            first_z(1, 0)
+    cross_other(0, 0)
+    cross_other(0, 1)
+    g_zph(R - 1)
     cross_y(1, 0)
-    cross_z(0, 0)
-
-    for i in range(R - 1):
-        g_z(i).wait_recv()
+    for b in bits:
+        g_z(b, b).wait_recv()
 
     eye = (
         lax.broadcasted_iota(jnp.int32, (D, D), 0) == lax.broadcasted_iota(jnp.int32, (D, D), 1)
     ).astype(jnp.float32)
     scales = []
+    tail = slice(hp * PACKED, hp * PACKED + PAD)
+    col_sums = gp[c, z, y, tail, :]
+    for b in bits:
+        col_sums = col_sums + gz[b - 1, tail, :]
     for j in range(hp):
-        total = gp[c, z, y, j]
-        for i in range(R - 1):
-            total = total + gz[i, j]
-        mean = total[PACKED:, :] / token_total
+        at = slice(j * PACKED, (j + 1) * PACKED)
+        total = gp[c, z, y, at, :]
+        for b in bits:
+            total = total + gz[b - 1, at, :]
+        mean = jnp.where(sub8 == 0, col_sums[j : j + 1, :], 0.0) / token_total
         slab[0, j, D:, :] = mean
-        cov = unpack(total[:PACKED, :]) / token_total - dot_tt(mean, mean, HI) * (1.0 / PAD) + ridge_weight * eye
+        cov = unpack(total) / token_total - dot_tt(mean, mean, HI) + ridge_weight * eye
         norm2 = jnp.sum(jnp.sum(cov * cov, axis=1, keepdims=True), axis=0, keepdims=True)
         scale = jnp.sqrt(norm2)
         scales.append(scale)
@@ -314,19 +442,19 @@
 
     def up(d):
         block = wbuf.at[c, z - d, y]
-        return rc(block, block, az_s.at[0, d], az_r.at[0, d], z_peer(z + 1), lay)
+        return rc(block, block, az_s.at[0, d], az_r.at[0, d], z_peer_at(z + 1), lay)
 
     def down(d):
         block = wbuf.at[c, z + d, y]
-        return rc(block, block, az_s.at[1, d], az_r.at[1, d], z_peer(z - 1), lay)
+        return rc(block, block, az_s.at[1, d], az_r.at[1, d], z_peer_at(z - 1), lay)
 
     def from_below(d):
         block = wbuf.at[c, z - d, y]
-        return rc(block, block, az_s.at[0, d - 1], az_r.at[0, d - 1], z_peer(z - 1), lay)
+        return rc(block, block, az_s.at[0, d - 1], az_r.at[0, d - 1], z_peer_at(z - 1), lay)
 
     def from_above(d):
         block = wbuf.at[c, z + d, y]
-        return rc(block, block, az_s.at[1, d - 1], az_r.at[1, d - 1], z_peer(z + 1), lay)
+        return rc(block, block, az_s.at[1, d - 1], az_r.at[1, d - 1], z_peer_at(z + 1), lay)
 
     def a_y(zs):
         block = wbuf.at[c, zs, y]
@@ -439,47 +567,83 @@
     def final(k):
         @pl.when(c == k)
         def _():
-            c_d(k, R - 1, 1).wait_recv()
+            to_core.wait_recv()
+            if k == 0:
+                f_y().wait_recv()
+            else:
+                to_lay.wait_recv()
             c_y(k, R - 1).wait_recv()
-            for i in range(R - 1):
-                c_z(k, i).wait_recv()
-            to_core.wait_recv()
+
+            def add(slot):
+                c_z_in(k, slot).wait_recv()
+                for j in range(zf if k == 0 else 0, hp):
+                    cp[k, z, y, j] = cp[k, z, y, j] + cz[slot, j]
+
+            sources(z, True, add)
+            for j in range(hp):
+                left = slab[k, j]
+                right = slab[1 + k, j]
+                if k == 0 and j < zf:
+                    total = cp[k, z, y, j] + cyf[j]
+                else:
+                    total = cp[k, z, y, j] + cy[z, j]
+                zb[j] = total / token_total - dot_tt(left[D:, :], right[D:, :], HI)
             if k == 1:
-                to_lay.wait_recv()
+                c_d(k, R - 1, 1).wait_recv()
+                for j in range(hp):
+                    zb[j] = zb[j] + cd[z, y, j] / token_total
+            for j in range(hp):
+                yb[j] = mm(slab[k, j, :D, :], zb[j])
+            for j in range(hp):
+                white = mm(yb[j], slab[1 + k, j, :D, :])
+                zb[j] = white * white
             tile = jnp.zeros(sbuf.shape[1:], jnp.float32)
             for j in range(hp):
-                total = cp[k, z, y, j] + cd[z, y, j] + cy[z, j]
-                for i in range(R - 1):
-                    total = total + cz[i, j]
-                left = slab[k, j]
-                right = slab[1 + k, j]
-                cross = total / token_total - dot_tt(left[D:, :], right[D:, :], HI) * (1.0 / PAD)
-                white = mm(mm(left[:D, :], cross), right[:D, :])
-                value = jnp.sum(jnp.sum(white * white, axis=1, keepdims=True), axis=0, keepdims=True) / HEAD_DIM
+                value = jnp.sum(jnp.sum(zb[j], axis=0, keepdims=True), axis=1, keepdims=True) / HEAD_DIM
                 tile = jnp.where(lane == group + j, value, tile)
             sbuf[me] = tile
             for q in range(1, n):
                 s_out(q).start()
 
-    todo = []
+    for i in range(R - 1):
+        cross_z(0, i, 0)
     for i in range(1, R - 1):
-        todo.append(lambda i=i: cross_z(0, i))
-    own_steps = todo
-
-    for f in own_steps:
-        f()
-    for i in range(1, R):
-        cross_other(i)
-        gather_z(i)
-        cross_y(1, i)
-        cross_z(1, i - 1)
-        expand_z(i)
-        gather_y(i - 1)
-        if i == R - 2 or R == 2:
-            final(0)
-        gather_core(i - 1, 1)
+        first_z(i, 1)
+        if i + 1 < R - 1:
+            first_z(i + 1, 0)
+    cross_z(1, 0, 0)
+    cross_other(1, 0)
+    cross_other(1, 1)
+    cross_y(1, 1)
+    gather_z(1)
+    for d in range(2, R - 1):
+        cross_other(d, 0)
+        cross_y(1, d)
+        gather_y(d - 2)
+        gather_z(d)
+        cross_other(d, 1)
+        for q in range(d - 2, R - 1 if d == R - 2 else d - 1):
+            cross_z(0, q, 1)
+        cross_z(1, d - 2, 1)
+        cross_z(1, d - 1, 0)
+        expand_z(d - 1)
+    gather_y(R - 3)
+    gather_z(R - 1)
+    cross_other(R - 1, 0)
+    cross_y(1, R - 1)
+    cross_z(1, R - 3, 1)
+    cross_z(1, R - 2, 0)
+    first_z(R - 1)
+    gather_y(R - 2)
+    final(0)
+    expand_z(R - 2)
+    expand_z(R - 1)
+    cross_z(1, R - 2, 1)
+    for d in range(R - 1):
+        gather_core(d, 1)
+    cross_other(R - 1, 1)
+    final(1)
     gather_y(R - 1)
-    final(1)
     gather_core(R - 1, 1)
     for d in range(R):
         gather_core(d, 0)
@@ -501,13 +665,25 @@
             g_d(i, half).wait_send()
             c_d(1 - c, i, half).wait_send()
         g_y(i).wait_send()
-        c_y(c, i).wait_send()
+        for k in range(2):
+            @pl.when(c == k)
+            def _():
+                c_y(k, i).wait_send()
+
         a_y(i).wait_send()
         for half in range(2):
             a_d(c, i, half).wait_send()
+    for o in range(1, R):
+        g_z(o, lowest(o)).wait_send()
     for i in range(R - 1):
-        g_z(i).wait_send()
-        c_z(c, i).wait_send()
+        zt = ct_of(i)
+        for k in range(2):
+            @pl.when(c == k)
+            def _():
+                c_z(k, zt, slot_of(zt)).wait_send()
+                if k == 0:
+                    f_z(zt, slot_of(zt)).wait_send()
+
     for d in range(R - 1):
         @when(jnp.logical_and(has_below(d), has_above(1)))
         def _():
@@ -518,6 +694,10 @@
             down(d).wait_send()
 
     to_core.wait_send()
+
+    @pl.when(c == 0)
+    def _():
+        f_y().wait_send()
 
     @pl.when(c == 1)
     def _():
@@ -531,8 +711,9 @@
     n = mesh.shape["tok"]
     R = n // 4
     hp = -(-HEADS // (n // 2))
+    zf = max(hp * Z_FIRST // 5, 1)
     D = HEAD_DIM
-    E = PACKED + PAD
+    E = hp * PACKED + PAD
     parts = 1 if R * 2 * hp != HEADS else 2 * R
 
     def local(first_acts, second_acts):
@@ -542,7 +723,7 @@
         bf16 = jnp.bfloat16
         dma = lambda *k: pltpu.SemaphoreType.DMA(tuple(max(q, 1) for q in k))
         out, sims = pl.pallas_call(
-            functools.partial(kernel, n, R, hp, token_total),
+            functools.partial(kernel, n, R, hp, zf, token_total),
             out_shape=(
                 pltpu.VMEM((2, R, 2, hp, D, D), f32),
                 pltpu.VMEM((2, HEADS), f32),
@@ -556,14 +737,16 @@
                 pltpu.VMEM((rows, width), bf16),
                 pltpu.VMEM((rows, width), bf16),
                 pltpu.VMEM((rows, width), bf16),
-                pltpu.VMEM((2, R, 2, hp, E, D), f32),
-                pltpu.VMEM((R, 2, hp, E, D), f32),
-                pltpu.VMEM((R, hp, E, D), f32),
-                pltpu.VMEM((R - 1, hp, E, D), f32),
+                pltpu.VMEM((2, R, 2, E, D), f32),
+                pltpu.VMEM((R, 2, E, D), f32),
+                pltpu.VMEM((R, E, D), f32),
+                pltpu.VMEM((R - 1, E, D), f32),
                 pltpu.VMEM((2, R, 2, hp, D, D), f32),
                 pltpu.VMEM((R, 2, hp, D, D), f32),
                 pltpu.VMEM((R, hp, D, D), f32),
-                pltpu.VMEM((R - 1, hp, D, D), f32),
+                pltpu.VMEM((R + 1, hp, D, D), f32),
+                pltpu.VMEM((zf, D, D), f32),
+                pltpu.VMEM((R + 1, 2, zf, D, D), f32),
                 pltpu.VMEM((3, hp, D + PAD, D), f32),
                 pltpu.VMEM((2, R, 2, hp, PACKED, D), f32),
                 pltpu.VMEM((n, 8, D), f32),
@@ -571,7 +754,7 @@
                 pltpu.VMEM((hp, D, D), f32),
                 dma(2 * parts), dma(parts), dma(parts),
                 dma(2, R), dma(2, R), dma(R), dma(R), dma(R - 1), dma(R - 1),
-                dma(2, R), dma(2, R), dma(R), dma(R), dma(R - 1), dma(R - 1),
+                dma(2, R), dma(2, R), dma(R), dma(R), dma(R + 1), dma(R + 1), dma(1), dma(1), dma(R + 1), dma(R + 1),
                 dma(1), dma(1), dma(1), dma(1),
                 dma(2, R), dma(2, R), dma(R), dma(R), dma(2, R), dma(2, R),
                 dma(n), dma(n),

time: 90.6 us -> 78.5 us (0.87)
  Pallas kernels: 86.9 us -> 74.8 us
    pallas_call x1, Pallas kernels: 86.9 us -> 74.8 us  [local(): pl.pallas_call(functools.partial(kernel, n, R, hp, zf, token_total), out_...]
where the time goes in v3:
time: 78.5 us; the launch traced here: 78.4 us
  Pallas kernels  74.8 us (95%)
  local copies, waits for them, and re-layouts  2.92 us (4%)
    pallas_call x1, Pallas kernels, local(): pl.pallas_call(functools.partial(kernel, n, R, hp, zf, token_total), out_...  74.8 us
    unnamed x2, local copies, waits for them, and re-layouts  2.92 us

profile of v3, /device:TPU:0, one launch (start us, length us, event | category | flops | bytes accessed | tf_op | source)
XLA Modules:
  0.0 78.4 jit_solution(83343449536411446)
XLA Ops:
  0.6 74.8 %shard_map.41 = (f32[2,4,2,5,128,128]{5,4,3,2,1,0:T(8,128)S(1)}, f32[2,40]{1,0:T(2,128)S(1)}) custom-call(bf16[256,5120]{1,0:T(8,128)(2,1)} %bitcast.8, bf16[256,5120]{1,0:T(8,128)(2,1)} %bitcast.9), custom_call_target="tpu_custom_call" | custom-call | tf_op jit(solution)/shard_map/pallas_call | solution.py:725
  75.5 2.4 %copy.7 = f32[2,1,40,128,128]{4,3,2,1,0:T(8,128)} copy(f32[2,1,40,128,128]{4,3,2,1,0:T(8,128)S(1)} %bitcast.6) | data formatting | bytes 10485760
  77.8 0.6 copy.8

commit v4 on v3

--- a/solution.py
+++ b/solution.py
@@ -69,7 +69,7 @@
 def kernel(
     n, R, hp, zf, token_total,
     x1h, x2h, out, simout,
-    x1, x2, x2o, gp, gd, gy, gz, cp, cd, cy, cz, cyf, czf, slab, wbuf, sbuf, yb, zb,
+    x1, x2, x2o, gp, gd, gy, gz, cp, cd, cy, cz, cyf, czf, slab, wlay, wbuf, sbuf, yb, zb,
     l_s, x_s, x_r, gd_s, gd_r, gy_s, gy_r, gz_s, gz_r,
     cd_s, cd_r, cy_s, cy_r, cz_s, cz_r, fy_s, fy_r, fz_s, fz_r,
     p_s, p_r, q_s, q_r, az_s, az_r, ay_s, ay_r, ad_s, ad_r, ss_s, ss_r,
@@ -162,25 +162,20 @@
         half = yn if p % 2 == 0 else y
         return pl.ds(pl.multiple_of((ct_of(p // 2) * 2 + half) * width, 128), width)
 
-    order = list(range(0, parts, 2)) + list(range(1, parts, 2))
-    loads = {}
-    for p in order:
-        cols = part_cols(p)
-        for k, (src, dst) in enumerate(((x2h, x2), (x1h, x1))):
-            d = pltpu.make_async_copy(src.at[:, cols], dst.at[:, cols], l_s.at[2 * p + k])
-            d.start()
-            loads[p, k] = d
+    load_x2 = pltpu.make_async_copy(x2h, x2, l_s.at[0])
+    load_x1 = pltpu.make_async_copy(x1h, x1, l_s.at[1])
+    load_x2.start()
+    load_x1.start()
 
     def x_send(p):
         cols = part_cols(p)
-        return rc(x2.at[:, cols], x2o.at[:, cols], x_s.at[p], x_r.at[p], me, other)
+        return rc(x2.at[:, cols], x2o.at[:, cols], x_s.at[0], x_r.at[p], me, other)
 
     pl.semaphore_wait(barrier, n)
+    load_x2.wait()
     for p in range(parts):
-        loads[p, 0].wait()
         x_send(p).start()
-    for p in range(parts):
-        loads[p, 1].wait()
+    load_x1.wait()
 
     def head_cols(zt, yy, j):
         h = (zt * 2 + yy) * hp + j
@@ -208,14 +203,14 @@
     def g_d(i, half):
         zt = zt_of(i)
         yy = yn if half == 0 else y
-        return rc(gp.at[1 - c, zt, yy], gd.at[zt, yy], gd_s.at[half, i], gd_r.at[half, i], core_peer, lay)
+        return rc(gp.at[1 - c, zt, yy], gd.at[zt, yy], gd_s.at[0], gd_r.at[half, i], core_peer, lay)
 
     def g_y(i):
         zt = zt_of(i)
-        return rc(gp.at[c, zt, yn], gy.at[zt], gy_s.at[i], gy_r.at[i], y_peer, lay)
+        return rc(gp.at[c, zt, yn], gy.at[zt], gy_s.at[0], gy_r.at[i], y_peer, lay)
 
     def g_z(o, b):
-        return rc(gp.at[c, z_xor(o), y], gz.at[o - 1], gz_s.at[o - 1], gz_r.at[o - 1], z_peer(b), lay)
+        return rc(gp.at[c, z_xor(o), y], gz.at[o - 1], gz_s.at[0], gz_r.at[o - 1], z_peer(b), lay)
 
     def g_yph(i):
         zt = zt_of(i)
@@ -261,7 +256,7 @@
     def c_d(k, i, half):
         zt = ct_of(i)
         yy = yn if half == 0 else y
-        return rc(cp.at[k, zt, yy], cd.at[zt, yy], cd_s.at[half, i], cd_r.at[half, i], core_peer, lay)
+        return rc(cp.at[k, zt, yy], cd.at[zt, yy], cd_s.at[0], cd_r.at[half, i], core_peer, lay)
 
     def own_heads(k):
         return pl.ds(zf, hp - zf) if k == 0 else pl.ds(0, hp)
@@ -269,23 +264,23 @@
     def c_y(k, i):
         zt = ct_of(i)
         hs = own_heads(k)
-        return rc(cp.at[k, zt, yn, hs], cy.at[zt, hs], cy_s.at[i], cy_r.at[i], y_peer, lay)
+        return rc(cp.at[k, zt, yn, hs], cy.at[zt, hs], cy_s.at[0], cy_r.at[i], y_peer, lay)
 
     def c_z(k, zt, slot):
         hs = own_heads(k)
-        return rc(cp.at[k, zt, y, hs], cz.at[slot, hs], cz_s.at[zt], cz_r.at[slot], z_peer_at(z + hop(zt)), lay)
+        return rc(cp.at[k, zt, y, hs], cz.at[slot, hs], cz_s.at[0], cz_r.at[slot], z_peer_at(z + hop(zt)), lay)
 
     def c_z_in(k, slot):
         hs = own_heads(k)
-        return rc(cp.at[k, z, y, hs], cz.at[slot, hs], cz_s.at[z], cz_r.at[slot], me, other)
+        return rc(cp.at[k, z, y, hs], cz.at[slot, hs], cz_s.at[0], cz_r.at[slot], me, other)
 
     def f_z(zt, slot):
         return rc(
-            cp.at[0, zt, :, pl.ds(0, zf)], czf.at[slot], fz_s.at[zt], fz_r.at[slot], z_peer_at(z + hop(zt)), lay
+            cp.at[0, zt, :, pl.ds(0, zf)], czf.at[slot], fz_s.at[0], fz_r.at[slot], z_peer_at(z + hop(zt)), lay
         )
 
     def f_z_in(slot):
-        return rc(cp.at[0, z, :, pl.ds(0, zf)], czf.at[slot], fz_s.at[z], fz_r.at[slot], me, other)
+        return rc(cp.at[0, z, :, pl.ds(0, zf)], czf.at[slot], fz_s.at[0], fz_r.at[slot], me, other)
 
     def f_y():
         return rc(cp.at[0, z, yn, pl.ds(0, zf)], cyf, fy_s.at[0], fy_r.at[0], y_peer, lay)
@@ -298,7 +293,7 @@
             pl.when(has_source(zt) == 1)(lambda: body(zt))
 
     def first_z(i, chained=None):
-        ready = c == 0
+        ready = c == 1
         if chained is not None:
             ready = jnp.logical_and(ready, has_source(ct_of(i)) == chained)
 
@@ -327,12 +322,12 @@
             cols = head_cols(zt, yy, j)
             cp[k, zt, yy, j] = dot_tt(x1[:, cols], ref[:, cols])
 
+        @pl.when(c == k)
+        def _():
+            c_d(k, i, half).start()
+
+    def cross_y(k, i):
         @pl.when(c == 1 - k)
-        def _():
-            c_d(k, i, half).start()
-
-    def cross_y(k, i):
-        @pl.when(c == k)
         def _():
             zt = ct_of(i)
             c_d(k, i, 0).wait_recv()
@@ -345,7 +340,7 @@
                     cp[k, zt, y, j] = cp[k, zt, y, j] + cd[zt, y, j]
 
     def cross_z(k, i, chained):
-        @pl.when(jnp.logical_and(c == k, has_source(ct_of(i)) == chained))
+        @pl.when(jnp.logical_and(c == 1 - k, has_source(ct_of(i)) == chained))
         def _():
             zt = ct_of(i)
             if k == 1:
@@ -458,18 +453,21 @@
 
     def a_y(zs):
         block = wbuf.at[c, zs, y]
-        return rc(block, block, ay_s.at[zs], ay_r.at[zs], y_peer, lay)
+        return rc(block, block, ay_s.at[0], ay_r.at[zs], y_peer, lay)
 
     def a_y_in(zs):
         block = wbuf.at[c, zs, yn]
-        return rc(block, block, ay_s.at[zs], ay_r.at[zs], y_peer, lay)
+        return rc(block, block, ay_s.at[0], ay_r.at[zs], y_peer, lay)
 
     def a_d(cc, zs, half):
         block = wbuf.at[cc, zs, yn if half == 0 else y]
-        return rc(block, block, ad_s.at[half, zs], ad_r.at[half, zs], core_peer, lay)
+        return rc(block, block, ad_s.at[0], ad_r.at[half, zs], core_peer, lay)
 
     to_core = rc(slab.at[0], slab.at[1], p_s.at[0], p_r.at[0], core_peer, lay)
-    to_lay = rc(slab.at[0], slab.at[2], q_s.at[0], q_r.at[0], me, other)
+    to_lay = [
+        rc(wbuf.at[1, z, y], wlay, q_s.at[0], q_r.at[0], core_peer, other),
+        rc(slab.at[0, :, pl.ds(D, PAD)], slab.at[2, :, pl.ds(D, PAD)], q_s.at[1], q_r.at[1], core_peer, other),
+    ]
 
     def has_below(d):
         return z - d >= 0
@@ -494,7 +492,8 @@
 
     @pl.when(c == 1)
     def _():
-        to_lay.start()
+        to_lay[1].start()
+        to_lay[0].start()
 
     def gather_z(d):
         @when(has_below(d))
@@ -558,20 +557,21 @@
     lane = lax.broadcasted_iota(jnp.int32, sbuf.shape[1:], 1)
 
     def s_out(k):
-        return rc(sbuf.at[me], sbuf.at[me], ss_s.at[k], ss_r.at[k], lax.rem(me + k, n), lay)
-
-    def s_in(k):
-        src = lax.rem(me + n - k, n)
-        return rc(sbuf.at[src], sbuf.at[src], ss_s.at[k], ss_r.at[k], src, lay)
+        return rc(sbuf.at[me], sbuf.at[me], ss_s.at[0], ss_r.at[0], lax.rem(me + k, n), lay)
 
     def final(k):
-        @pl.when(c == k)
+        left_at, right_at = (1, 0) if k == 0 else (0, 2)
+
+        @pl.when(c == 1 - k)
         def _():
             to_core.wait_recv()
             if k == 0:
                 f_y().wait_recv()
             else:
-                to_lay.wait_recv()
+                for d in to_lay[::-1]:
+                    d.wait_recv()
+                for j in range(hp):
+                    slab[2, j, :D, :] = unpack(wlay[j])
             c_y(k, R - 1).wait_recv()
 
             def add(slot):
@@ -581,8 +581,8 @@
 
             sources(z, True, add)
             for j in range(hp):
-                left = slab[k, j]
-                right = slab[1 + k, j]
+                left = slab[left_at, j]
+                right = slab[right_at, j]
                 if k == 0 and j < zf:
                     total = cp[k, z, y, j] + cyf[j]
                 else:
@@ -593,9 +593,9 @@
                 for j in range(hp):
                     zb[j] = zb[j] + cd[z, y, j] / token_total
             for j in range(hp):
-                yb[j] = mm(slab[k, j, :D, :], zb[j])
+                yb[j] = mm(slab[left_at, j, :D, :], zb[j])
             for j in range(hp):
-                white = mm(yb[j], slab[1 + k, j, :D, :])
+                white = mm(yb[j], slab[right_at, j, :D, :])
                 zb[j] = white * white
             tile = jnp.zeros(sbuf.shape[1:], jnp.float32)
             for j in range(hp):
@@ -627,84 +627,73 @@
         cross_z(1, d - 2, 1)
         cross_z(1, d - 1, 0)
         expand_z(d - 1)
+    gather_z(R - 1)
+    cross_z(1, R - 2, 0)
     gather_y(R - 3)
-    gather_z(R - 1)
     cross_other(R - 1, 0)
     cross_y(1, R - 1)
     cross_z(1, R - 3, 1)
-    cross_z(1, R - 2, 0)
+    cross_z(1, R - 2, 1)
     first_z(R - 1)
     gather_y(R - 2)
-    final(0)
     expand_z(R - 2)
     expand_z(R - 1)
-    cross_z(1, R - 2, 1)
     for d in range(R - 1):
         gather_core(d, 1)
     cross_other(R - 1, 1)
+    final(0)
     final(1)
     gather_y(R - 1)
     gather_core(R - 1, 1)
     for d in range(R):
         gather_core(d, 0)
 
-    for k in range(1, n):
-        s_in(k).wait_recv()
+    def sent(ref, sem):
+        rc(ref, ref, sem.at[0], sem.at[0], core_peer, lay).wait_send()
+
+    sent(x2, x_s)
+    sent(gd, gd_s)
+    sent(gy, gy_s)
+    sent(gz, gz_s)
+    sent(cd, cd_s)
+    sent(wbuf.at[c, :, y], ay_s)
+    sent(wbuf.at[c], ad_s)
+    for k in range(2):
+        @pl.when(c == 1 - k)
+        def _():
+            hs = own_heads(k)
+            sent(cy.at[:, hs], cy_s)
+            sent(cz.at[pl.ds(0, R - 1), hs], cz_s)
+            if k == 0:
+                sent(czf.at[pl.ds(0, R - 1)], fz_s)
+                f_y().wait_send()
+
+    for d in range(R - 1):
+        @when(jnp.logical_and(has_below(d), has_above(1)))
+        def _():
+            up(d).wait_send()
+
+        @when(jnp.logical_and(has_above(d), has_below(1)))
+        def _():
+            down(d).wait_send()
+
+    to_core.wait_send()
+
+    @pl.when(c == 1)
+    def _():
+        for d in to_lay:
+            d.wait_send()
+
+    tiles = sbuf.at[pl.ds(0, n - 1)]
+    sent(tiles, ss_s)
+    rc(tiles, tiles, ss_s.at[0], ss_r.at[0], core_peer, lay).wait_recv()
     row0 = sbuf[0]
     row1 = sbuf[1]
     for i in range(2, n, 2):
         row0 = row0 + sbuf[i]
         row1 = row1 + sbuf[i + 1]
     sub = lax.broadcasted_iota(jnp.int32, row0.shape, 0)
-    simout[...] = jnp.where(sub == lay, row0, row1)[:2, :HEADS]
-
-    for p in range(parts):
-        x_send(p).wait_send()
-    for i in range(R):
-        for half in range(2):
-            g_d(i, half).wait_send()
-            c_d(1 - c, i, half).wait_send()
-        g_y(i).wait_send()
-        for k in range(2):
-            @pl.when(c == k)
-            def _():
-                c_y(k, i).wait_send()
-
-        a_y(i).wait_send()
-        for half in range(2):
-            a_d(c, i, half).wait_send()
-    for o in range(1, R):
-        g_z(o, lowest(o)).wait_send()
-    for i in range(R - 1):
-        zt = ct_of(i)
-        for k in range(2):
-            @pl.when(c == k)
-            def _():
-                c_z(k, zt, slot_of(zt)).wait_send()
-                if k == 0:
-                    f_z(zt, slot_of(zt)).wait_send()
-
-    for d in range(R - 1):
-        @when(jnp.logical_and(has_below(d), has_above(1)))
-        def _():
-            up(d).wait_send()
-
-        @when(jnp.logical_and(has_above(d), has_below(1)))
-        def _():
-            down(d).wait_send()
-
-    to_core.wait_send()
-
-    @pl.when(c == 0)
-    def _():
-        f_y().wait_send()
-
-    @pl.when(c == 1)
-    def _():
-        to_lay.wait_send()
-
-    for k in range(1, n):
-        s_out(k).wait_send()
+    simout[...] = jnp.where(sub == lay, row1, row0)[:2, :HEADS]
 
 
 def solution(mesh):
@@ -748,16 +737,18 @@
                 pltpu.VMEM((zf, D, D), f32),
                 pltpu.VMEM((R + 1, 2, zf, D, D), f32),
                 pltpu.VMEM((3, hp, D + PAD, D), f32),
+                pltpu.VMEM((hp, PACKED, D), f32),
                 pltpu.VMEM((2, R, 2, hp, PACKED, D), f32),
                 pltpu.VMEM((n, 8, D), f32),
                 pltpu.VMEM((hp, D, D), f32),
                 pltpu.VMEM((hp, D, D), f32),
-                dma(2 * parts), dma(parts), dma(parts),
-                dma(2, R), dma(2, R), dma(R), dma(R), dma(R - 1), dma(R - 1),
-                dma(2, R), dma(2, R), dma(R), dma(R), dma(R + 1), dma(R + 1), dma(1), dma(1), dma(R + 1), dma(R + 1),
-                dma(1), dma(1), dma(1), dma(1),
-                dma(2, R), dma(2, R), dma(R), dma(R), dma(2, R), dma(2, R),
-                dma(n), dma(n),
+                dma(2), dma(1), dma(parts),
+                dma(1), dma(2, R), dma(1), dma(R), dma(1), dma(R - 1),
+                dma(1), dma(2, R), dma(1), dma(R), dma(1), dma(R + 1),
+                dma(1), dma(1), dma(1), dma(R + 1),
+                dma(1), dma(1), dma(2), dma(2),
+                dma(2, R - 1), dma(2, R - 1), dma(1), dma(R), dma(1), dma(2, R),
+                dma(1), dma(1),
             ],
             compiler_params=pltpu.CompilerParams(
                 collective_id=0, has_side_effects=True, vmem_limit_bytes=VMEM_LIMIT

time: 78.5 us -> 76.7 us (0.977)
  Pallas kernels: 74.8 us -> 73 us
    pallas_call x1, Pallas kernels: 74.8 us -> 73 us  [local(): pl.pallas_call(functools.partial(kernel, n, R, hp, zf, token_total), out_...]
where the time goes in v4:
time: 76.7 us; the launch traced here: 76.6 us
  Pallas kernels  73 us (95%)
  local copies, waits for them, and re-layouts  2.92 us (4%)
    pallas_call x1, Pallas kernels, local(): pl.pallas_call(functools.partial(kernel, n, R, hp, zf, token_total), out_...  73 us
    unnamed x2, local copies, waits for them, and re-layouts  2.92 us

profile of v4, /device:TPU:0, one launch (start us, length us, event | category | flops | bytes accessed | tf_op | source)
XLA Modules:
  0.0 76.6 jit_solution(7808249758714166672)
XLA Ops:
  0.6 73.0 %shard_map.41 = (f32[2,4,2,5,128,128]{5,4,3,2,1,0:T(8,128)S(1)}, f32[2,40]{1,0:T(2,128)S(1)}) custom-call(bf16[256,5120]{1,0:T(8,128)(2,1)} %bitcast.8, bf16[256,5120]{1,0:T(8,128)(2,1)} %bitcast.9), custom_call_target="tpu_custom_call" | custom-call | tf_op jit(solution)/shard_map/pallas_call | solution.py:714
  73.6 2.4 %copy.7 = f32[2,1,40,128,128]{4,3,2,1,0:T(8,128)} copy(f32[2,1,40,128,128]{4,3,2,1,0:T(8,128)S(1)} %bitcast.6) | data formatting | bytes 10485760
  76.0 0.6 copy.8

commit v5 on v4

--- a/solution.py
+++ b/solution.py
@@ -31,7 +31,7 @@
 
 BLOCKS = HEAD_DIM // 8
 KEPT = BLOCKS // 2 + 1
-PACKED = 8 * KEPT
+MAIN = 8 * (KEPT - 1)
 
 
 def lane_block():
@@ -49,7 +49,26 @@
     return jnp.concatenate([xs[(-d) % BLOCKS] for d in range(KEPT)], axis=0)
 
 
-def unpack(p):
+def packed_rows(hp):
+    return hp * MAIN + (hp + 1) // 2 * 8
+
+
+def store_packed(ref, blocks):
+    hp = len(blocks)
+    first = lax.broadcasted_iota(jnp.int32, (8, HEAD_DIM), 1) < HEAD_DIM // 2
+    for j in range(hp):
+        ref[j * MAIN : (j + 1) * MAIN, :] = blocks[j][:MAIN, :]
+    for t in range((hp + 1) // 2):
+        left, right = blocks[2 * t], blocks[min(2 * t + 1, hp - 1)]
+        ref[hp * MAIN + 8 * t : hp * MAIN + 8 * t + 8, :] = jnp.where(first, left[MAIN:, :], right[MAIN:, :])
+
+
+def load_packed(read, hp, j):
+    at = hp * MAIN + 8 * (j // 2)
+    return unpack(jnp.concatenate([read(j * MAIN, (j + 1) * MAIN), read(at, at + 8)], axis=0), j % 2)
+
+
+def unpack(p, odd):
     lb = lane_block()
     zero = jnp.zeros((8, HEAD_DIM), jnp.float32)
     ys = [zero] * BLOCKS
@@ -63,7 +82,10 @@
     half = jnp.concatenate(ys, axis=0)
     rb = lax.broadcasted_iota(jnp.int32, (HEAD_DIM, HEAD_DIM), 0) // 8
     cb = lax.broadcasted_iota(jnp.int32, (HEAD_DIM, HEAD_DIM), 1) // 8
-    return jnp.where((cb - rb + BLOCKS) % BLOCKS < KEPT, half, half.T)
+    away = (cb - rb + BLOCKS) % BLOCKS
+    side = cb >= BLOCKS // 2 if odd else cb < BLOCKS // 2
+    keep = jnp.logical_or(away < KEPT - 1, jnp.logical_and(away == KEPT - 1, side))
+    return jnp.where(keep, half, half.T)
 
 
 def kernel(
@@ -190,14 +212,16 @@
         zt = zt_of(i)
         yy = yn if half == 0 else y
         sums = [jnp.zeros((PAD, D), jnp.float32)] * 2
+        blocks = [[], []]
         for j in range(hp):
             cols = head_cols(zt, yy, j)
             for k, ref in enumerate((x1, x2)):
                 v = ref[:, cols]
-                gp[k, zt, yy, j * PACKED : (j + 1) * PACKED, :] = pack(dot_tt(v, v))
+                blocks[k].append(pack(dot_tt(v, v)))
                 sums[k] = jnp.where(sub8 == j, jnp.dot(ones, v, preferred_element_type=jnp.float32), sums[k])
         for k in range(2):
-            gp[k, zt, yy, hp * PACKED :, :] = sums[k]
+            store_packed(gp.at[k, zt, yy], blocks[k])
+            gp[k, zt, yy, packed_rows(hp) :, :] = sums[k]
         g_d(i, half).start()
 
     def g_d(i, half):
@@ -400,18 +424,20 @@
         lax.broadcasted_iota(jnp.int32, (D, D), 0) == lax.broadcasted_iota(jnp.int32, (D, D), 1)
     ).astype(jnp.float32)
     scales = []
-    tail = slice(hp * PACKED, hp * PACKED + PAD)
+    tail = slice(packed_rows(hp), packed_rows(hp) + PAD)
     col_sums = gp[c, z, y, tail, :]
     for b in bits:
         col_sums = col_sums + gz[b - 1, tail, :]
     for j in range(hp):
-        at = slice(j * PACKED, (j + 1) * PACKED)
-        total = gp[c, z, y, at, :]
-        for b in bits:
-            total = total + gz[b - 1, at, :]
+        def read(lo, hi):
+            total = gp[c, z, y, lo:hi, :]
+            for b in bits:
+                total = total + gz[b - 1, lo:hi, :]
+            return total
+
         mean = jnp.where(sub8 == 0, col_sums[j : j + 1, :], 0.0) / token_total
         slab[0, j, D:, :] = mean
-        cov = unpack(total) / token_total - dot_tt(mean, mean, HI) + ridge_weight * eye
+        cov = load_packed(read, hp, j) / token_total - dot_tt(mean, mean, HI) + ridge_weight * eye
         norm2 = jnp.sum(jnp.sum(cov * cov, axis=1, keepdims=True), axis=0, keepdims=True)
         scale = jnp.sqrt(norm2)
         scales.append(scale)
@@ -428,12 +454,14 @@
         return carry
 
     lax.fori_loop(1, ITERS - 1, ns_body, 0)
+    factors = []
     for j in range(hp):
         f = 1.5 * eye - 0.5 * mm(zb[j], yb[j])
         w = mm(f, zb[j]) / jnp.sqrt(scales[j])
         slab[0, j, :D, :] = w
-        wbuf[c, z, y, j] = pack(w)
         out[c, z, y, j] = w
+        factors.append(pack(w))
+    store_packed(wbuf.at[c, z, y], factors)
 
     def up(d):
         block = wbuf.at[c, z - d, y]
@@ -520,7 +548,7 @@
 
     def expand(cc, zs, yy):
         for j in range(hp):
-            out[cc, zs, yy, j] = unpack(wbuf[cc, zs, yy, j])
+            out[cc, zs, yy, j] = load_packed(lambda lo, hi: wbuf[cc, zs, yy, lo:hi, :], hp, j)
 
     def sides(d, body):
         if d == 0:
@@ -571,7 +599,7 @@
                 for d in to_lay[::-1]:
                     d.wait_recv()
                 for j in range(hp):
-                    slab[2, j, :D, :] = unpack(wlay[j])
+                    slab[2, j, :D, :] = load_packed(lambda lo, hi: wlay[lo:hi, :], hp, j)
             c_y(k, R - 1).wait_recv()
 
             def add(slot):
@@ -696,13 +724,24 @@
     simout[...] = jnp.where(sub == lay, row1, row0)[:2, :HEADS]
 
 
+def write_out(white, sims, white_out, sims_out, sem):
+    copies = [pltpu.make_async_copy(sims, sims_out, sem.at[0])]
+    for k in range(2):
+        for i in range(white.shape[1]):
+            copies.append(pltpu.make_async_copy(white.at[k, i], white_out.at[k, i], sem.at[len(copies)]))
+    for d in copies:
+        d.start()
+    for d in copies:
+        d.wait()
+
+
 def solution(mesh):
     n = mesh.shape["tok"]
     R = n // 4
     hp = -(-HEADS // (n // 2))
     zf = max(hp * Z_FIRST // 5, 1)
     D = HEAD_DIM
-    E = hp * PACKED + PAD
+    E = packed_rows(hp) + PAD
     parts = 1 if R * 2 * hp != HEADS else 2 * R
 
     def local(first_acts, second_acts):
@@ -737,8 +776,8 @@
                 pltpu.VMEM((zf, D, D), f32),
                 pltpu.VMEM((R + 1, 2, zf, D, D), f32),
                 pltpu.VMEM((3, hp, D + PAD, D), f32),
-                pltpu.VMEM((hp, PACKED, D), f32),
-                pltpu.VMEM((2, R, 2, hp, PACKED, D), f32),
+                pltpu.VMEM((E - PAD, D), f32),
+                pltpu.VMEM((2, R, 2, E - PAD, D), f32),
                 pltpu.VMEM((n, 8, D), f32),
                 pltpu.VMEM((hp, D, D), f32),
                 pltpu.VMEM((hp, D, D), f32),
@@ -754,6 +793,17 @@
                 collective_id=0, has_side_effects=True, vmem_limit_bytes=VMEM_LIMIT
             ),
         )(first_acts[0], second_acts[0])
+        out, sims = pl.pallas_call(
+            write_out,
+            out_shape=(
+                jax.ShapeDtypeStruct((2, R, 2, hp, D, D), f32),
+                jax.ShapeDtypeStruct((2, HEADS), f32),
+            ),
+            in_specs=[pl.BlockSpec(memory_space=pl.ANY)] * 2,
+            out_specs=(pl.BlockSpec(memory_space=pltpu.MemorySpace.HBM),) * 2,
+            scratch_shapes=[dma(2 * R + 1)],
+            compiler_params=pltpu.CompilerParams(vmem_limit_bytes=1024 * 1024),
+        )(out, sims)
         whitening = out.reshape(2, R * 2 * hp, D, D)[:, None, :HEADS]
         return whitening, sims[None]
 

time: 76.7 us -> 75.7 us (0.987)
  local copies, waits for them, and re-layouts: 2.92 us -> 0 us
  Pallas kernels: 73 us -> 74.8 us
    unnamed x2 -> x0, local copies, waits for them, and re-layouts: 2.92 us -> none
    pallas_call x0 -> x1, Pallas kernels: none -> 2.43 us  [local(): pl.pallas_call(write_out, out_shape=(jax.ShapeDtypeStruct((2, R, 2, hp, D...]
where the time goes in v5:
time: 75.7 us; the launch traced here: 75.6 us
  Pallas kernels  74.8 us (99%)
  between operations  0.8 us (1%)
    pallas_call x1, Pallas kernels, local(): pl.pallas_call(functools.partial(kernel, n, R, hp, zf, token_total), out_...  72.4 us
    pallas_call x1, Pallas kernels, local(): pl.pallas_call(write_out, out_shape=(jax.ShapeDtypeStruct((2, R, 2, hp, D...  2.43 us

profile of v5, /device:TPU:0, one launch (start us, length us, event | category | flops | bytes accessed | tf_op | source)
XLA Modules:
  0.0 75.6 jit_solution(17451785261002154139)
XLA Ops:
  0.6 72.4 %shard_map.41 = (f32[2,4,2,5,128,128]{5,4,3,2,1,0:T(8,128)S(1)}, f32[2,40]{1,0:T(2,128)S(1)}) custom-call(bf16[256,5120]{1,0:T(8,128)(2,1)} %bitcast.6, bf16[256,5120]{1,0:T(8,128)(2,1)} %bitcast.7), custom_call_target="tpu_custom_call" | custom-call | tf_op jit(solution)/shard_map/pallas_call | solution.py:753
  73.0 2.4 %shard_map.42 = (f32[2,4,2,5,128,128]{5,4,3,2,1,0:T(8,128)}, f32[2,40]{1,0:T(2,128)}) custom-call(f32[2,4,2,5,128,128]{5,4,3,2,1,0:T(8,128)S(1)} %get-tuple-element.6.white, f32[2,40]{1,0:T(2,128)S(1)} %get-tuple-element.7.sims), custom_call_target="tpu_custom_call" | custom-call | tf_op jit(solution)/shard_map/pallas_call | solution.py:796

commit v6 on v5

--- a/solution.py
+++ b/solution.py
@@ -596,10 +596,7 @@
             if k == 0:
                 f_y().wait_recv()
             else:
-                for d in to_lay[::-1]:
-                    d.wait_recv()
-                for j in range(hp):
-                    slab[2, j, :D, :] = load_packed(lambda lo, hi: wlay[lo:hi, :], hp, j)
+                to_lay[1].wait_recv()
             c_y(k, R - 1).wait_recv()
 
             def add(slot):
@@ -622,6 +619,10 @@
                     zb[j] = zb[j] + cd[z, y, j] / token_total
             for j in range(hp):
                 yb[j] = mm(slab[left_at, j, :D, :], zb[j])
+            if k == 1:
+                to_lay[0].wait_recv()
+                for j in range(hp):
+                    slab[2, j, :D, :] = load_packed(lambda lo, hi: wlay[lo:hi, :], hp, j)
             for j in range(hp):
                 white = mm(yb[j], slab[right_at, j, :D, :])
                 zb[j] = white * white

time: 75.7 us -> 75.2 us (level)
  no operation moved by 1% of the time
where the time goes in v6:
time: 75.2 us; the launch traced here: 75.1 us
  Pallas kernels  74.3 us (99%)
  between operations  0.8 us (1%)
    pallas_call x1, Pallas kernels, local(): pl.pallas_call(functools.partial(kernel, n, R, hp, zf, token_total), out_...  71.9 us
    pallas_call x1, Pallas kernels, local(): pl.pallas_call(write_out, out_shape=(jax.ShapeDtypeStruct((2, R, 2, hp, D...  2.43 us

profile of v6, /device:TPU:0, one launch (start us, length us, event | category | flops | bytes accessed | tf_op | source)
XLA Modules:
  0.0 75.1 jit_solution(3524700279731508385)
XLA Ops:
  0.6 71.9 %shard_map.41 = (f32[2,4,2,5,128,128]{5,4,3,2,1,0:T(8,128)S(1)}, f32[2,40]{1,0:T(2,128)S(1)}) custom-call(bf16[256,5120]{1,0:T(8,128)(2,1)} %bitcast.6, bf16[256,5120]{1,0:T(8,128)(2,1)} %bitcast.7), custom_call_target="tpu_custom_call" | custom-call | tf_op jit(solution)/shard_map/pallas_call | solution.py:754
  72.5 2.4 %shard_map.42 = (f32[2,4,2,5,128,128]{5,4,3,2,1,0:T(8,128)}, f32[2,40]{1,0:T(2,128)}) custom-call(f32[2,4,2,5,128,128]{5,4,3,2,1,0:T(8,128)S(1)} %get-tuple-element.6.white, f32[2,40]{1,0:T(2,128)S(1)} %get-tuple-element.7.sims), custom_call_target="tpu_custom_call" | custom-call | tf_op jit(solution)/shard_map/pallas_call | solution.py:797
